TPU v7x, 256 devices: a 8x8x2 block of a 8x8x16 slice. The times are simulated.
256 devices in a mesh: shot: 2 (over z), gy: 128 (over x, y, core).
Axes of the slice: x: 8, y: 8, z: 2, core: 2. Of those that a mesh axis runs over, the one named last changes fastest.
The devices are a block of a 8x8x16 slice.
Arguments:
- source_now: float32 [32, 1024, 256], P('shot', 'gy'), parts along dimension 0, may hold values from -4 to 4
- source_before: float32 [32, 1024, 256], P('shot', 'gy'), parts along dimension 0, may hold values from -4 to 4
- receiver_now: float32 [32, 1024, 256], P('shot', 'gy'), parts along dimension 0, may hold values from -4 to 4
- receiver_before: float32 [32, 1024, 256], P('shot', 'gy'), parts along dimension 0, may hold values from -4 to 4
- speed_term: float32 [16, 1024, 256], P(None, 'gy'), may hold values from 0.03 to 0.12
- aniso_field: float32 [16, 1024, 256], P(None, 'gy'), may hold values from 0 to 0.3
- tilt_field: float32 [16, 1024, 256], P(None, 'gy'), may hold values from -0.5 to 0.5
- angle_bins: int32 [16, 1024, 256], P(None, 'gy'), may hold values from 0 to 7
- weight_table: bfloat16 [24, 8, 4], replicated, may hold values from -1.25 to 1.25
- offset_lags: int32 [24], replicated, may hold values from -16 to 16, as said below
- source_cells: int32 [16], P('shot'), parts along dimension 0, may hold values from 0 to 262143
- source_wavelet: float32 [4, 8], P('shot'), parts along dimension 0, may hold values from -24 to 24
- receiver_cells: int32 [4096], P('shot'), parts along dimension 0, may hold values from 0 to 262143
- receiver_traces: float32 [4, 2048], P('shot'), parts along dimension 0, may hold values from -18 to 18
Outputs:
- angle_images: bfloat16 [8, 16, 1024, 256], P('shot', None, 'gy'), parts along dimension 0
There are 2 independent parts, one for each index of `shot`. A program takes and returns all parts, laid end to end along the dimension named above; an argument that names none is the same for every part. Nothing has to cross between parts.
Inputs may be any that keep to these rules, and one draw needn't show every extreme that they name: `offset_lags`: 24 distinct lags; -16 and 16 are among them.
All inputs are finite; a program needn't handle non-finite values.
Results may differ from a plain program's by a relative error of at most 0.0051.
Values may be sent and summed in bfloat16 or wider, within the bound.
A program may use at most 64 MiB of HBM per device.

v0:
```python
import functools

import jax
import jax.numpy as jnp
from jax import lax
from jax.experimental import pallas as pl
from jax.experimental.pallas import tpu as pltpu
from jax.sharding import PartitionSpec as P

SECOND_COEF = (-205.0 / 72.0, 8.0 / 5.0, -1.0 / 5.0, 8.0 / 315.0, -1.0 / 560.0)
FIRST_COEF = (4.0 / 5.0, -1.0 / 5.0, 4.0 / 105.0, -1.0 / 280.0)
MESH = pl.DeviceIdType.MESH
F32 = jnp.float32
BF16 = jnp.bfloat16
LANES = 128
ROWS = 8
PAD = 4
LO, HI = 0, 1
OFFSETS = (-2, -1, 1, 2)


def kernel(
    sn_hbm, sb_hbm, rn_hbm, rb_hbm, speed_hbm, aniso_hbm, tilt_hbm, bins_hbm, wt_hbm,
    lags, scells, swave, rcells_hbm, rtraces_hbm,
    out_hbm,
    pw, qv, speed, a1, a2, bins, wt, rcells, rtraces, table, inj, base, grad,
    send0, send1, send2, recv0, recv1, recv2, win, acc, outv,
    in_sem, out_sem, send_sem0, recv_sem0, send_sem1, recv_sem1, send_sem2, recv_sem2,
):
    n = lax.axis_size("gy")
    me = lax.axis_index("gy")
    peer = {d: lax.rem(me + (d + n), n) for d in OFFSETS}
    zs = sn_hbm.shape[0]
    halves = sn_hbm.shape[2] // LANES
    n_off, n_bin, n_ang = wt_hbm.shape
    steps = swave.shape[0]
    n_src = scells.shape[0]
    rec_rows = rcells_hbm.shape[0]
    own = pl.ds(ROWS, ROWS)
    inner = pl.ds(PAD, zs)

    barrier = pltpu.get_barrier_semaphore()
    for d in OFFSETS:
        pl.semaphore_signal(barrier, inc=1, device_id={"gy": peer[d]}, device_id_type=MESH)

    copies = {}

    def fetch(name, index, src, dst):
        copy = pltpu.make_async_copy(src, dst, in_sem.at[index])
        copy.start()
        copies[name] = copy

    count = 0
    for m, ref in enumerate((sn_hbm, rn_hbm)):
        for x in range(halves):
            fetch(("now", m, x), count, ref.at[:, :, pl.ds(x * LANES, LANES)], pw.at[0, m, x, inner, own, :])
            count += 1
    for m, ref in enumerate((sb_hbm, rb_hbm)):
        for x in range(halves):
            fetch(("before", m, x), count, ref.at[:, :, pl.ds(x * LANES, LANES)], qv.at[m, x])
            count += 1
    for name, ref, dst in (("speed", speed_hbm, speed), ("aniso", aniso_hbm, a1), ("tilt", tilt_hbm, a2), ("bins", bins_hbm, bins)):
        for x in range(halves):
            fetch((name, x), count, ref.at[:, :, pl.ds(x * LANES, LANES)], dst.at[x])
            count += 1
    fetch("rcells", count, rcells_hbm, rcells)
    fetch("rtraces", count + 1, rtraces_hbm, rtraces)
    fetch("wt", count + 2, wt_hbm, wt)

    sub = lax.broadcasted_iota(jnp.int32, (ROWS, LANES), 0)
    lane = lax.broadcasted_iota(jnp.int32, (ROWS, LANES), 1)
    low_rows = sub < PAD

    def turn(v):
        return pltpu.roll(v, PAD, axis=v.ndim - 2)

    def pack(source, receiver, send, x, where_z):
        send[LO, x, where_z] = jnp.where(low_rows, source, turn(receiver)).astype(BF16)
        send[HI, x, where_z] = jnp.where(low_rows, turn(source), receiver).astype(BF16)

    def remote(src, dst, ssem, rsem, d):
        return pltpu.make_async_remote_copy(
            src_ref=src, dst_ref=dst, send_sem=ssem, recv_sem=rsem, device_id={"gy": peer[d]}, device_id_type=MESH
        )

    edge = jnp.zeros((PAD, ROWS, LANES), F32)
    for x in range(halves):
        for m in range(2):
            for s in range(steps):
                pw[s, m, x, pl.ds(0, PAD), own, :] = edge
                pw[s, m, x, pl.ds(PAD + zs, PAD), own, :] = edge
            grad[m, x, pl.ds(0, PAD)] = edge
            grad[m, x, pl.ds(PAD + zs, PAD)] = edge

    for m in range(2):
        for x in range(halves):
            copies[("now", m, x)].wait()
    for x in range(halves):
        pack(pw[0, 0, x, inner, own, :], pw[0, 1, x, inner, own, :], send0, x, pl.ds(0, zs))

    pl.semaphore_wait(barrier, len(OFFSETS))

    halo = [
        remote(send0.at[HI], recv0.at[0], send_sem0.at[0], recv_sem0.at[0], 1),
        remote(send0.at[LO], recv0.at[1], send_sem0.at[1], recv_sem0.at[1], -1),
    ]
    for copy in halo:
        copy.start()

    for x in range(halves):
        copies[("speed", x)].wait()
        copies[("aniso", x)].wait()
        copies[("tilt", x)].wait()
        a1[x] = speed[x] * (1.0 + 2.0 * a1[x])
        a2[x] = speed[x] * a2[x]

    def local_part(step):
        chunk = 2

        def part(i, carry):
            z = i * chunk
            for m in range(2):
                f = [pw[step, m, x, pl.ds(PAD + z, chunk), own, :] for x in range(halves)]
                first = [jnp.zeros_like(v) for v in f]
                second = [SECOND_COEF[0] * v for v in f]
                for k in range(1, PAD + 1):
                    up = [pltpu.roll(v, LANES - k, axis=2) for v in f] + [jnp.zeros_like(f[0])]
                    down = [jnp.zeros_like(f[0])] + [pltpu.roll(v, k, axis=2) for v in f]
                    for x in range(halves):
                        above = jnp.where(lane < LANES - k, up[x], up[x + 1])
                        below = jnp.where(lane >= k, down[x + 1], down[x])
                        second[x] = second[x] + SECOND_COEF[k] * (above + below)
                        first[x] = first[x] + FIRST_COEF[k - 1] * (above - below)
                for x in range(halves):
                    grad[m, x, pl.ds(PAD + z, chunk)] = first[x]
                    along_z = SECOND_COEF[0] * f[x]
                    for k in range(1, PAD + 1):
                        along_z = along_z + SECOND_COEF[k] * (
                            pw[step, m, x, pl.ds(PAD + z + k, chunk), own, :]
                            + pw[step, m, x, pl.ds(PAD + z - k, chunk), own, :]
                        )
                    before = qv[m, x, pl.ds(z, chunk)] if step == 0 else pw[step - 1, m, x, pl.ds(PAD + z, chunk), own, :]
                    base[m, x, pl.ds(z, chunk)] = (
                        2.0 * f[x]
                        - before
                        + a1[x, pl.ds(z, chunk)] * second[x]
                        + speed[x, pl.ds(z, chunk)] * along_z
                    )
            return carry

        lax.fori_loop(0, zs // chunk, part, 0)
        for m in range(2):
            for x in range(halves):
                base[m, x, 0] = base[m, x, 0] + inj[step, m, x]

    def injections():
        first_row = me * ROWS
        copies["rcells"].wait()
        copies["rtraces"].wait()
        left, right = [], []
        col_iota = lax.broadcasted_iota(jnp.int32, (halves * LANES, LANES), 0)
        for c in range(rec_rows):
            cell = rcells[c : c + 1, :]
            row = lax.shift_right_logical(cell, shift_bits) - first_row
            col = jnp.bitwise_and(cell, halves * LANES - 1)
            hit = jnp.broadcast_to(row, (ROWS, LANES)) == sub
            parts = []
            for s in range(steps):
                amount = jnp.broadcast_to(rtraces[s : s + 1, c * LANES : (c + 1) * LANES], (ROWS, LANES))
                amount = jnp.where(hit, amount, 0.0)
                coarse = amount.astype(BF16).astype(F32)
                parts += [coarse, amount - coarse]
            left.append(jnp.concatenate(parts, axis=0).astype(BF16))
            right.append(jnp.where(jnp.broadcast_to(col, col_iota.shape) == col_iota, 1.0, 0.0).astype(BF16))
        spread = lax.dot_general(
            jnp.concatenate(left, axis=1),
            jnp.concatenate(right, axis=1),
            (((1,), (1,)), ((), ())),
            preferred_element_type=F32,
        )
        for s in range(steps):
            total = spread[2 * s * ROWS : (2 * s + 1) * ROWS] + spread[(2 * s + 1) * ROWS : (2 * s + 2) * ROWS]
            for x in range(halves):
                inj[s, 1, x] = total[:, x * LANES : (x + 1) * LANES]
        for s in range(steps):
            for x in range(halves):
                total = jnp.zeros((ROWS, LANES), F32)
                for i in range(n_src):
                    cell = scells[i]
                    row = lax.shift_right_logical(cell, shift_bits) - first_row
                    col = jnp.bitwise_and(cell, halves * LANES - 1) - x * LANES
                    total = total + jnp.where((sub == row) & (lane == col), swave[s, i], 0.0)
                inj[s, 0, x] = total

    shift_bits = (halves * LANES).bit_length() - 1

    def halo_rows(step, below, above):
        for x in range(halves):
            low = below[x].astype(F32)
            high = above[x].astype(F32)
            pw[step, 0, x, inner, pl.ds(0, ROWS), :] = turn(low)
            pw[step, 1, x, inner, pl.ds(0, ROWS), :] = low
            pw[step, 0, x, inner, pl.ds(2 * ROWS, ROWS), :] = high
            pw[step, 1, x, inner, pl.ds(2 * ROWS, ROWS), :] = turn(high)

    def y_part(step, send):
        chunk = 4

        def along_y(i, carry):
            z = i * chunk
            for m in range(2):
                for x in range(halves):
                    def rows(k):
                        return pw[step, m, x, pl.ds(PAD + z, chunk), pl.ds(ROWS + k, ROWS), :]

                    second = SECOND_COEF[0] * rows(0)
                    first = grad[m, x, pl.ds(PAD + z, chunk)]
                    for k in range(1, PAD + 1):
                        above, below = rows(k), rows(-k)
                        second = second + SECOND_COEF[k] * (above + below)
                        first = first + FIRST_COEF[k - 1] * (above - below)
                    grad[m, x, pl.ds(PAD + z, chunk)] = first
                    base[m, x, pl.ds(z, chunk)] = base[m, x, pl.ds(z, chunk)] + a1[x, pl.ds(z, chunk)] * second
            return carry

        lax.fori_loop(0, zs // chunk, along_y, 0)

        def finish(i, carry):
            z = i * chunk
            for x in range(halves):
                new = []
                for m in range(2):
                    mixed = jnp.zeros((chunk, ROWS, LANES), F32)
                    for k in range(1, PAD + 1):
                        mixed = mixed + FIRST_COEF[k - 1] * (
                            grad[m, x, pl.ds(PAD + z + k, chunk)] - grad[m, x, pl.ds(PAD + z - k, chunk)]
                        )
                    value = base[m, x, pl.ds(z, chunk)] + a2[x, pl.ds(z, chunk)] * mixed
                    new.append(value)
                    if step + 1 < steps:
                        pw[step + 1, m, x, pl.ds(PAD + z, chunk), own, :] = value
                    win[step, m, x, pl.ds(z, chunk), pl.ds(2 * ROWS, ROWS), :] = value.astype(BF16).astype(F32)
                pack(new[0], new[1], send, x, pl.ds(z, chunk))
            return carry

        lax.fori_loop(0, zs // chunk, finish, 0)

    def open_block(step, d, recv):
        slot = OFFSETS.index(d)
        rows = pl.ds((2 + d) * ROWS, ROWS)
        for x in range(halves):
            low = recv[slot, LO, x].astype(F32)
            high = recv[slot, HI, x].astype(F32)
            win[step, 0, x, :, rows, :] = jnp.where(low_rows, low, turn(high))
            win[step, 1, x, :, rows, :] = jnp.where(low_rows, turn(low), high)

    chunk = 4
    groups = zs // chunk

    def image(step, last):
        def part(i, carry):
            x = i // groups
            z = lax.rem(i, groups) * chunk
            bin_ids = [bins[x, z + j] for j in range(chunk)]
            if step == 0:
                total = [[jnp.zeros((ROWS, LANES), F32)] * chunk for a in range(n_ang)]
            else:
                total = [[acc[a, x, z + j] for j in range(chunk)] for a in range(n_ang)]
            for h in range(n_off):
                lag = lags[h]
                product = (
                    win[step, 0, x, pl.ds(z, chunk), pl.ds(2 * ROWS - lag, ROWS), :]
                    * win[step, 1, x, pl.ds(z, chunk), pl.ds(2 * ROWS + lag, ROWS), :]
                )
                for a in range(n_ang):
                    weights = table[h, a]
                    for j in range(chunk):
                        weight = jnp.take_along_axis(weights, bin_ids[j], axis=0)
                        total[a][j] = total[a][j] + weight * product[j]
            for a in range(n_ang):
                for j in range(chunk):
                    if last:
                        outv[x, a, z + j] = total[a][j].astype(BF16)
                    else:
                        acc[a, x, z + j] = total[a][j]
            return carry

        lax.fori_loop(0, halves * groups, part, 0)

    injections()
    for m in range(2):
        for x in range(halves):
            copies[("before", m, x)].wait()
    local_part(0)
    copies["wt"].wait()
    for h in range(n_off):
        weights = wt[h].astype(F32)
        for a in range(n_ang):
            table[h, a] = jnp.broadcast_to(weights[:, a : a + 1], (n_bin, LANES))
    for x in range(halves):
        copies[("bins", x)].wait()

    for copy in halo:
        copy.wait_recv()
    halo_rows(0, recv0.at[0], recv0.at[1])
    y_part(0, send1)

    first = {}
    for index, (half, d) in enumerate(((HI, 1), (LO, -1), (LO, 1), (HI, -1))):
        slot = OFFSETS.index(-d)
        first[(half, d)] = remote(
            send1.at[half], recv1.at[slot, half], send_sem1.at[index], recv_sem1.at[index], d
        )
        first[(half, d)].start()
    for index, d in ((4, 2), (5, -2)):
        first[d] = remote(send1, recv1.at[OFFSETS.index(-d)], send_sem1.at[index], recv_sem1.at[index], d)
        first[d].start()

    local_part(1)
    first[(HI, 1)].wait_recv()
    first[(LO, -1)].wait_recv()
    halo_rows(1, recv1.at[OFFSETS.index(-1), HI], recv1.at[OFFSETS.index(1), LO])
    y_part(1, send2)

    second = {}
    for index, d in enumerate((2, -2, 1, -1)):
        second[d] = remote(send2, recv2.at[OFFSETS.index(-d)], send_sem2.at[index], recv_sem2.at[index], d)
        second[d].start()

    first[(LO, 1)].wait_recv()
    first[(HI, -1)].wait_recv()
    first[2].wait_recv()
    first[-2].wait_recv()
    for d in OFFSETS:
        open_block(0, d, recv1)
    image(0, False)

    for d in (1, -1, 2, -2):
        second[d].wait_recv()
        open_block(1, -d, recv2)
    image(1, True)

    writes = [
        pltpu.make_async_copy(outv.at[x], out_hbm.at[:, :, :, pl.ds(x * LANES, LANES)], out_sem.at[x])
        for x in range(halves)
    ]
    for copy in writes:
        copy.start()
    for copy in writes:
        copy.wait()
    for copy in halo + list(first.values()) + list(second.values()):
        copy.wait_send()


def per_device(
    source_now, source_before, receiver_now, receiver_before, speed_term, aniso_field, tilt_field,
    angle_bins, weight_table, offset_lags, source_cells, source_wavelet, receiver_cells, receiver_traces,
):
    zs, rows, width = source_now.shape
    halves = width // LANES
    steps = source_wavelet.shape[0]
    n_off, n_bin, n_ang = weight_table.shape
    receivers = receiver_cells.shape[0]
    assert rows == ROWS and n_bin == ROWS and width & (width - 1) == 0
    half = (halves, zs, ROWS, LANES)
    any_space = pl.BlockSpec(memory_space=pl.ANY)
    smem = pl.BlockSpec(memory_space=pltpu.SMEM)
    dma = pltpu.SemaphoreType.DMA
    in_specs = [any_space] * 9 + [smem] * 3 + [any_space] * 2
    return pl.pallas_call(
        kernel,
        out_shape=jax.ShapeDtypeStruct((n_ang, zs, rows, width), BF16),
        in_specs=in_specs,
        out_specs=any_space,
        scratch_shapes=[
            pltpu.VMEM((steps, 2, halves, zs + 2 * PAD, 3 * ROWS, LANES), F32),
            pltpu.VMEM((2,) + half, F32),
            pltpu.VMEM(half, F32),
            pltpu.VMEM(half, F32),
            pltpu.VMEM(half, F32),
            pltpu.VMEM(half, jnp.int32),
            pltpu.VMEM((n_off, n_bin, n_ang), BF16),
            pltpu.VMEM((receivers // LANES, LANES), jnp.int32),
            pltpu.VMEM((steps, receivers), F32),
            pltpu.VMEM((n_off, n_ang, n_bin, LANES), F32),
            pltpu.VMEM((steps, 2, halves, ROWS, LANES), F32),
            pltpu.VMEM((2,) + half, F32),
            pltpu.VMEM((2, halves, zs + 2 * PAD, ROWS, LANES), F32),
            pltpu.VMEM((2,) + half, BF16),
            pltpu.VMEM((2,) + half, BF16),
            pltpu.VMEM((2,) + half, BF16),
            pltpu.VMEM((2,) + half, BF16),
            pltpu.VMEM((len(OFFSETS), 2) + half, BF16),
            pltpu.VMEM((len(OFFSETS), 2) + half, BF16),
            pltpu.VMEM((steps, 2, halves, zs, 5 * ROWS, LANES), F32),
            pltpu.VMEM((n_ang,) + half, F32),
            pltpu.VMEM((halves, n_ang, zs, ROWS, LANES), BF16),
            dma((8 * halves + 3,)),
            dma((halves,)),
            dma((2,)),
            dma((2,)),
            dma((6,)),
            dma((6,)),
            dma((4,)),
            dma((4,)),
        ],
        compiler_params=pltpu.CompilerParams(collective_id=0, has_side_effects=True),
    )(
        source_now, source_before, receiver_now, receiver_before, speed_term, aniso_field, tilt_field,
        angle_bins, weight_table, offset_lags, source_cells, source_wavelet,
        receiver_cells.reshape(receivers // LANES, LANES), receiver_traces,
    )


def solution(mesh):
    return jax.shard_map(
        per_device,
        mesh=mesh,
        in_specs=(
            P("shot", "gy", None),
            P("shot", "gy", None),
            P("shot", "gy", None),
            P("shot", "gy", None),
            P(None, "gy", None),
            P(None, "gy", None),
            P(None, "gy", None),
            P(None, "gy", None),
            P(),
            P(),
            P("shot"),
            P("shot", None),
            P("shot"),
            P("shot", None),
        ),
        out_specs=P("shot", None, "gy", None),
        check_vma=False,
    )
```

profile of v0, /device:TPU:513, one launch (start us, length us, event | category | flops | bytes accessed | tf_op | source)
XLA Modules:
  0.0 44.8 jit_solution(14599137643292090391)
XLA Ops:
  0.0 1.5 %copy.15.wt_hbm = bf16[24,8,4]{2,1,0:T(8,128)(2,1)} copy(bf16[24,8,4]{0,2,1:T(4,128)(2,1)} %param.22) | data formatting | bytes 3072 | tf_op args[8]
  1.5 41.6 %shard_map.136 = bf16[4,16,8,256]{3,2,1,0:T(8,128)(2,1)} custom-call(f32[16,8,256]{2,1,0:T(8,128)} %sn_hbm.1, f32[16,8,256]{2,1,0:T(8,128)} %sb_hbm.1, f32[16,8,256]{2,1,0:T(8,128)} %rn_hbm.1, f32[16,8,256]{2,1,0:T(8,128)} %rb_hbm.1, f32[16,8,256]{2,1,0:T(8,128)} %speed_hbm.1, f32[16,8,256]{2,1,0:T(8,128)} %aniso_hbm.1, f32[16,8,256]{2,1,0:T(8,128)} %tilt_hbm.1, ...), custom_call_target="tpu_custom_call" | custom-call | tf_op jit(solution)/shard_map/pallas_call | solution.py:370
  43.1 1.7 %copy.17 = bf16[4,16,8,256]{3,2,1,0:T(8,128)(2,1)} copy(bf16[4,16,8,256]{3,2,1,0:T(8,128)(2,1)} %shard_map.136) | data formatting | bytes 524288
where the time goes:
time: 45 us; the launch traced here: 44.8 us
  Pallas kernels  41.6 us (92%)
  local copies, waits for them, and re-layouts  3.12 us (7%)
    pallas_call x1, Pallas kernels, per_device(): pl.pallas_call(kernel, out_shape=jax.ShapeDtypeStruct((n_ang, zs, rows, w...  41.6 us
    unnamed x2, local copies, waits for them, and re-layouts  3.12 us

commit v1 on v0

v1 whole, which is shorter than its diff:
```python
import functools

import jax
import jax.numpy as jnp
from jax import lax
from jax.experimental import pallas as pl
from jax.experimental.pallas import tpu as pltpu
from jax.sharding import PartitionSpec as P

SECOND_COEF = (-205.0 / 72.0, 8.0 / 5.0, -1.0 / 5.0, 8.0 / 315.0, -1.0 / 560.0)
FIRST_COEF = (4.0 / 5.0, -1.0 / 5.0, 4.0 / 105.0, -1.0 / 280.0)
MESH = pl.DeviceIdType.MESH
F32 = jnp.float32
BF16 = jnp.bfloat16
LANES = 128
ROWS = 8
PAD = 4
LO, HI = 0, 1
OFFSETS = (-2, -1, 1, 2)


def kernel(
    sn_hbm, sb_hbm, rn_hbm, rb_hbm, speed_hbm, aniso_hbm, tilt_hbm, bins_hbm, wt_hbm,
    lags_hbm, scells_hbm, swave_hbm, rcells_hbm, rtraces_hbm,
    out,
    pw, qv, speed, a1, a2, bins, wt, lags, scells, swave, rcells, rtraces, table, cache, inj, base, grad,
    send0, send1, send2, recv0, recv1, recv2, win, acc,
    in_sem, send_sem0, recv_sem0, send_sem1, recv_sem1, send_sem2, recv_sem2,
):
    n = lax.axis_size("gy")
    me = lax.axis_index("gy")
    peer = {d: lax.rem(me + (d + n), n) for d in OFFSETS}
    zs = sn_hbm.shape[0]
    halves = sn_hbm.shape[2] // LANES
    n_bin, n_ang, n_off = wt_hbm.shape
    steps = swave.shape[0]
    n_src = scells.shape[0]
    rec_rows = rcells_hbm.shape[0]
    own = pl.ds(ROWS, ROWS)
    inner = pl.ds(PAD, zs)

    barrier = pltpu.get_barrier_semaphore()
    for d in OFFSETS:
        pl.semaphore_signal(barrier, inc=1, device_id={"gy": peer[d]}, device_id_type=MESH)

    copies = {}

    def fetch(name, index, src, dst):
        copy = pltpu.make_async_copy(src, dst, in_sem.at[index])
        copy.start()
        copies[name] = copy

    count = 0
    for m, ref in enumerate((sn_hbm, rn_hbm)):
        for x in range(halves):
            fetch(("now", m, x), count, ref.at[:, :, pl.ds(x * LANES, LANES)], pw.at[0, m, x, inner, own, :])
            count += 1
    for m, ref in enumerate((sb_hbm, rb_hbm)):
        for x in range(halves):
            fetch(("before", m, x), count, ref.at[:, :, pl.ds(x * LANES, LANES)], qv.at[m, x])
            count += 1
    for name, ref, dst in (("speed", speed_hbm, speed), ("aniso", aniso_hbm, a1), ("tilt", tilt_hbm, a2), ("bins", bins_hbm, bins)):
        for x in range(halves):
            fetch((name, x), count, ref.at[:, :, pl.ds(x * LANES, LANES)], dst.at[x])
            count += 1
    fetch("rcells", count, rcells_hbm, rcells)
    fetch("rtraces", count + 1, rtraces_hbm, rtraces)
    fetch("wt", count + 2, wt_hbm, wt)
    fetch("lags", count + 3, lags_hbm, lags)
    fetch("scells", count + 4, scells_hbm, scells)
    fetch("swave", count + 5, swave_hbm, swave)

    sub = lax.broadcasted_iota(jnp.int32, (ROWS, LANES), 0)
    lane = lax.broadcasted_iota(jnp.int32, (ROWS, LANES), 1)
    low_rows = sub < PAD

    def turn(v):
        return pltpu.roll(v, PAD, axis=v.ndim - 2)

    def pack(source, receiver, send, x, where_z):
        send[x, LO, where_z] = jnp.where(low_rows, source, turn(receiver)).astype(BF16)
        send[x, HI, where_z] = jnp.where(low_rows, turn(source), receiver).astype(BF16)

    def remote(src, dst, ssem, rsem, d):
        return pltpu.make_async_remote_copy(
            src_ref=src, dst_ref=dst, send_sem=ssem, recv_sem=rsem, device_id={"gy": peer[d]}, device_id_type=MESH
        )

    halo = [
        (
            remote(send0.at[x, HI], recv0.at[x, 0], send_sem0.at[2 * x], recv_sem0.at[2 * x], 1),
            remote(send0.at[x, LO], recv0.at[x, 1], send_sem0.at[2 * x + 1], recv_sem0.at[2 * x + 1], -1),
        )
        for x in range(halves)
    ]
    for x in range(halves):
        for m in range(2):
            copies[("now", m, x)].wait()
        pack(pw[0, 0, x, inner, own, :], pw[0, 1, x, inner, own, :], send0, x, pl.ds(0, zs))
        if x == 0:
            pl.semaphore_wait(barrier, len(OFFSETS))
        for copy in halo[x]:
            copy.start()

    edge = jnp.zeros((PAD, ROWS, LANES), F32)
    for x in range(halves):
        for m in range(2):
            for s in range(steps):
                pw[s, m, x, pl.ds(0, PAD), own, :] = edge
                pw[s, m, x, pl.ds(PAD + zs, PAD), own, :] = edge
            grad[m, x, pl.ds(0, PAD)] = edge
            grad[m, x, pl.ds(PAD + zs, PAD)] = edge

    for x in range(halves):
        copies[("speed", x)].wait()
        copies[("aniso", x)].wait()
        copies[("tilt", x)].wait()
        a1[x] = speed[x] * (1.0 + 2.0 * a1[x])
        a2[x] = speed[x] * a2[x]

    def local_part(step):
        chunk = 2

        def part(i, carry):
            z = i * chunk
            for m in range(2):
                f = [pw[step, m, x, pl.ds(PAD + z, chunk), own, :] for x in range(halves)]
                first = [jnp.zeros_like(v) for v in f]
                second = [SECOND_COEF[0] * v for v in f]
                for k in range(1, PAD + 1):
                    up = [pltpu.roll(v, LANES - k, axis=2) for v in f] + [jnp.zeros_like(f[0])]
                    down = [jnp.zeros_like(f[0])] + [pltpu.roll(v, k, axis=2) for v in f]
                    for x in range(halves):
                        above = jnp.where(lane < LANES - k, up[x], up[x + 1])
                        below = jnp.where(lane >= k, down[x + 1], down[x])
                        second[x] = second[x] + SECOND_COEF[k] * (above + below)
                        first[x] = first[x] + FIRST_COEF[k - 1] * (above - below)
                for x in range(halves):
                    grad[m, x, pl.ds(PAD + z, chunk)] = first[x]
                    along_z = SECOND_COEF[0] * f[x]
                    for k in range(1, PAD + 1):
                        along_z = along_z + SECOND_COEF[k] * (
                            pw[step, m, x, pl.ds(PAD + z + k, chunk), own, :]
                            + pw[step, m, x, pl.ds(PAD + z - k, chunk), own, :]
                        )
                    before = qv[m, x, pl.ds(z, chunk)] if step == 0 else pw[step - 1, m, x, pl.ds(PAD + z, chunk), own, :]
                    base[m, x, pl.ds(z, chunk)] = (
                        2.0 * f[x]
                        - before
                        + a1[x, pl.ds(z, chunk)] * second[x]
                        + speed[x, pl.ds(z, chunk)] * along_z
                    )
            return carry

        lax.fori_loop(0, zs // chunk, part, 0)
        for m in range(2):
            for x in range(halves):
                base[m, x, 0] = base[m, x, 0] + inj[step, m, x]

    def injections():
        first_row = me * ROWS
        for name in ("rcells", "rtraces", "scells", "swave"):
            copies[name].wait()
        left, right = [], []
        col_iota = lax.broadcasted_iota(jnp.int32, (halves * LANES, LANES), 0)
        for c in range(rec_rows):
            cell = rcells[c : c + 1, :]
            row = lax.shift_right_logical(cell, shift_bits) - first_row
            col = jnp.bitwise_and(cell, halves * LANES - 1)
            hit = jnp.broadcast_to(row, (ROWS, LANES)) == sub
            parts = []
            for s in range(steps):
                amount = jnp.broadcast_to(rtraces[s : s + 1, c * LANES : (c + 1) * LANES], (ROWS, LANES))
                amount = jnp.where(hit, amount, 0.0)
                coarse = amount.astype(BF16).astype(F32)
                parts += [coarse, amount - coarse]
            left.append(jnp.concatenate(parts, axis=0).astype(BF16))
            right.append(jnp.where(jnp.broadcast_to(col, col_iota.shape) == col_iota, 1.0, 0.0).astype(BF16))
        spread = lax.dot_general(
            jnp.concatenate(left, axis=1),
            jnp.concatenate(right, axis=1),
            (((1,), (1,)), ((), ())),
            preferred_element_type=F32,
        )
        for s in range(steps):
            total = spread[2 * s * ROWS : (2 * s + 1) * ROWS] + spread[(2 * s + 1) * ROWS : (2 * s + 2) * ROWS]
            for x in range(halves):
                inj[s, 1, x] = total[:, x * LANES : (x + 1) * LANES]
        for s in range(steps):
            for x in range(halves):
                total = jnp.zeros((ROWS, LANES), F32)
                for i in range(n_src):
                    cell = scells[i]
                    row = lax.shift_right_logical(cell, shift_bits) - first_row
                    col = jnp.bitwise_and(cell, halves * LANES - 1) - x * LANES
                    total = total + jnp.where((sub == row) & (lane == col), swave[s, i], 0.0)
                inj[s, 0, x] = total

    shift_bits = (halves * LANES).bit_length() - 1

    def halo_rows(step, x, below, above):
        low = below[...].astype(F32)
        high = above[...].astype(F32)
        pw[step, 0, x, inner, pl.ds(0, ROWS), :] = turn(low)
        pw[step, 1, x, inner, pl.ds(0, ROWS), :] = low
        pw[step, 0, x, inner, pl.ds(2 * ROWS, ROWS), :] = high
        pw[step, 1, x, inner, pl.ds(2 * ROWS, ROWS), :] = turn(high)

    def y_part(step, x, send):
        chunk = 4

        def along_y(i, carry):
            z = i * chunk
            for m in range(2):

                def rows(k):
                    return pw[step, m, x, pl.ds(PAD + z, chunk), pl.ds(ROWS + k, ROWS), :]

                second = SECOND_COEF[0] * rows(0)
                first = grad[m, x, pl.ds(PAD + z, chunk)]
                for k in range(1, PAD + 1):
                    above, below = rows(k), rows(-k)
                    second = second + SECOND_COEF[k] * (above + below)
                    first = first + FIRST_COEF[k - 1] * (above - below)
                grad[m, x, pl.ds(PAD + z, chunk)] = first
                base[m, x, pl.ds(z, chunk)] = base[m, x, pl.ds(z, chunk)] + a1[x, pl.ds(z, chunk)] * second
            return carry

        lax.fori_loop(0, zs // chunk, along_y, 0)

        def finish(i, carry):
            z = i * chunk
            new = []
            for m in range(2):
                mixed = jnp.zeros((chunk, ROWS, LANES), F32)
                for k in range(1, PAD + 1):
                    mixed = mixed + FIRST_COEF[k - 1] * (
                        grad[m, x, pl.ds(PAD + z + k, chunk)] - grad[m, x, pl.ds(PAD + z - k, chunk)]
                    )
                value = base[m, x, pl.ds(z, chunk)] + a2[x, pl.ds(z, chunk)] * mixed
                new.append(value)
                if step + 1 < steps:
                    pw[step + 1, m, x, pl.ds(PAD + z, chunk), own, :] = value
                win[step, m, x, pl.ds(z, chunk), pl.ds(2 * ROWS, ROWS), :] = value.astype(BF16).astype(F32)
            pack(new[0], new[1], send, x, pl.ds(z, chunk))
            return carry

        lax.fori_loop(0, zs // chunk, finish, 0)

    def open_block(step, x, d, recv):
        slot = OFFSETS.index(d)
        rows = pl.ds((2 + d) * ROWS, ROWS)
        low = recv[slot, x, LO].astype(F32)
        high = recv[slot, x, HI].astype(F32)
        win[step, 0, x, :, rows, :] = jnp.where(low_rows, low, turn(high))
        win[step, 1, x, :, rows, :] = jnp.where(low_rows, turn(low), high)

    chunk = 4
    groups = zs // chunk

    def image(step, x):
        def part(i, carry):
            z = i * chunk
            if step == 0:
                bin_ids = [bins[x, z + j] for j in range(chunk)]
                total = [jnp.zeros((chunk, ROWS, LANES), F32)] * n_ang
            else:
                total = [acc[a, x, pl.ds(z, chunk)] for a in range(n_ang)]
            for h in range(n_off):
                lag = lags[h]
                product = (
                    win[step, 0, x, pl.ds(z, chunk), pl.ds(2 * ROWS - lag, ROWS), :]
                    * win[step, 1, x, pl.ds(z, chunk), pl.ds(2 * ROWS + lag, ROWS), :]
                )
                for a in range(n_ang):
                    if step == 0:
                        row = table[h, a]
                        weight = jnp.stack([jnp.take_along_axis(row, bin_ids[j], axis=0) for j in range(chunk)])
                        cache[h, a, x, pl.ds(z, chunk)] = weight
                    else:
                        weight = cache[h, a, x, pl.ds(z, chunk)]
                    total[a] = total[a] + weight * product
            for a in range(n_ang):
                if step + 1 == steps:
                    out[a, pl.ds(z, chunk), :, x * LANES : (x + 1) * LANES] = total[a].astype(BF16)
                else:
                    acc[a, x, pl.ds(z, chunk)] = total[a]
            return carry

        lax.fori_loop(0, groups, part, 0)

    for m in range(2):
        for x in range(halves):
            copies[("before", m, x)].wait()
    injections()
    local_part(0)
    copies["wt"].wait()
    copies["lags"].wait()
    by_bin = [wt[b].astype(F32) for b in range(n_bin)]
    for a in range(n_ang):
        rows = jnp.concatenate([v[a : a + 1] for v in by_bin], axis=0)
        for h in range(n_off):
            table[h, a] = jnp.broadcast_to(rows[:, h : h + 1], (n_bin, LANES))
    for x in range(halves):
        copies[("bins", x)].wait()

    slot_of = {d: OFFSETS.index(-d) for d in OFFSETS}
    border = []
    for x in range(halves):
        for copy in halo[x]:
            copy.wait_recv()
        halo_rows(0, x, recv0.at[x, 0], recv0.at[x, 1])
        y_part(0, x, send1)
        border.append(
            [
                remote(send1.at[x, half], recv1.at[slot_of[d], x, half], send_sem1.at[2 * x + i], recv_sem1.at[2 * x + i], d)
                for i, (half, d) in enumerate(((HI, 1), (LO, -1)))
            ]
        )
        for copy in border[x]:
            copy.start()
    rest = [
        remote(send1.at[:, half], recv1.at[slot_of[d], :, half], send_sem1.at[2 * halves + i], recv_sem1.at[2 * halves + i], d)
        for i, (half, d) in enumerate(((LO, 1), (HI, -1)))
    ] + [
        remote(send1, recv1.at[slot_of[d]], send_sem1.at[2 * halves + 2 + i], recv_sem1.at[2 * halves + 2 + i], d)
        for i, d in enumerate((2, -2))
    ]
    for copy in rest:
        copy.start()

    local_part(1)
    final = []
    for x in range(halves):
        for copy in border[x]:
            copy.wait_recv()
        halo_rows(1, x, recv1.at[slot_of[1], x, HI], recv1.at[slot_of[-1], x, LO])
        y_part(1, x, send2)
        final.append(
            [
                remote(send2.at[x], recv2.at[slot_of[d], x], send_sem2.at[4 * x + i], recv_sem2.at[4 * x + i], d)
                for i, d in enumerate((2, -2, 1, -1))
            ]
        )
        for copy in final[x]:
            copy.start()

    for copy in rest:
        copy.wait_recv()
    for x in range(halves):
        for d in OFFSETS:
            open_block(0, x, d, recv1)
        image(0, x)

    for x in range(halves):
        for copy in final[x]:
            copy.wait_recv()
        for d in OFFSETS:
            open_block(1, x, d, recv2)
        image(1, x)

    for copy in sum([list(c) for c in halo + border + final], []) + rest:
        copy.wait_send()


def per_device(
    source_now, source_before, receiver_now, receiver_before, speed_term, aniso_field, tilt_field,
    angle_bins, weight_table, offset_lags, source_cells, source_wavelet, receiver_cells, receiver_traces,
):
    zs, rows, width = source_now.shape
    halves = width // LANES
    steps = source_wavelet.shape[0]
    n_off, n_bin, n_ang = weight_table.shape
    n_src = source_cells.shape[0]
    receivers = receiver_cells.shape[0]
    assert rows == ROWS and n_bin == ROWS and width & (width - 1) == 0
    half = (halves, zs, ROWS, LANES)
    block = (halves, 2, zs, ROWS, LANES)
    any_space = pl.BlockSpec(memory_space=pl.ANY)
    dma = pltpu.SemaphoreType.DMA
    in_specs = [any_space] * 14
    return pl.pallas_call(
        kernel,
        out_shape=pltpu.VMEM((n_ang, zs, rows, width), BF16),
        in_specs=in_specs,
        out_specs=pl.BlockSpec(memory_space=pltpu.VMEM),
        scratch_shapes=[
            pltpu.VMEM((steps, 2, halves, zs + 2 * PAD, 3 * ROWS, LANES), F32),
            pltpu.VMEM((2,) + half, F32),
            pltpu.VMEM(half, F32),
            pltpu.VMEM(half, F32),
            pltpu.VMEM(half, F32),
            pltpu.VMEM(half, jnp.int32),
            pltpu.VMEM((n_bin, n_ang, n_off), BF16),
            pltpu.SMEM((n_off,), jnp.int32),
            pltpu.SMEM((n_src,), jnp.int32),
            pltpu.SMEM((steps, n_src), F32),
            pltpu.VMEM((receivers // LANES, LANES), jnp.int32),
            pltpu.VMEM((steps, receivers), F32),
            pltpu.VMEM((n_off, n_ang, n_bin, LANES), F32),
            pltpu.VMEM((n_off, n_ang) + half, F32),
            pltpu.VMEM((steps, 2, halves, ROWS, LANES), F32),
            pltpu.VMEM((2,) + half, F32),
            pltpu.VMEM((2, halves, zs + 2 * PAD, ROWS, LANES), F32),
            pltpu.VMEM(block, BF16),
            pltpu.VMEM(block, BF16),
            pltpu.VMEM(block, BF16),
            pltpu.VMEM(block, BF16),
            pltpu.VMEM((len(OFFSETS),) + block, BF16),
            pltpu.VMEM((len(OFFSETS),) + block, BF16),
            pltpu.VMEM((steps, 2, halves, zs, 5 * ROWS, LANES), F32),
            pltpu.VMEM((n_ang,) + half, F32),
            dma((8 * halves + 6,)),
            dma((2 * halves,)),
            dma((2 * halves,)),
            dma((2 * halves + 4,)),
            dma((2 * halves + 4,)),
            dma((4 * halves,)),
            dma((4 * halves,)),
        ],
        compiler_params=pltpu.CompilerParams(collective_id=0, has_side_effects=True),
    )(
        source_now, source_before, receiver_now, receiver_before, speed_term, aniso_field, tilt_field,
        angle_bins, jnp.transpose(weight_table, (1, 2, 0)), offset_lags, source_cells, source_wavelet,
        receiver_cells.reshape(receivers // LANES, LANES), receiver_traces,
    )


def solution(mesh):
    return jax.shard_map(
        per_device,
        mesh=mesh,
        in_specs=(
            P("shot", "gy", None),
            P("shot", "gy", None),
            P("shot", "gy", None),
            P("shot", "gy", None),
            P(None, "gy", None),
            P(None, "gy", None),
            P(None, "gy", None),
            P(None, "gy", None),
            P(),
            P(),
            P("shot"),
            P("shot", None),
            P("shot"),
            P("shot", None),
        ),
        out_specs=P("shot", None, "gy", None),
        check_vma=False,
    )
```

time: 45 us -> 39.3 us (0.87)
  Pallas kernels: 41.6 us -> 38.5 us
  local copies, waits for them, and re-layouts: 3.12 us -> 0.71 us
    pallas_call x1, Pallas kernels: 41.6 us -> 38.5 us  [per_device(): pl.pallas_call(kernel, out_shape=pltpu.VMEM((n_ang, zs, rows, width), BF1...]
    unnamed x2 -> x1, local copies, waits for them, and re-layouts: 3.12 us -> 0.71 us
where the time goes in v1:
time: 39.3 us; the launch traced here: 39.2 us
  Pallas kernels  38.5 us (98%)
  local copies, waits for them, and re-layouts  0.71 us (2%)
    pallas_call x1, Pallas kernels, per_device(): pl.pallas_call(kernel, out_shape=pltpu.VMEM((n_ang, zs, rows, width), BF1...  38.5 us

profile of v1, /device:TPU:513, one launch (start us, length us, event | category | flops | bytes accessed | tf_op | source)
XLA Modules:
  0.0 39.2 jit_solution(8037067309322790643)
XLA Ops:
  0.0 38.5 %shard_map.136 = bf16[4,16,8,256]{3,2,1,0:T(8,128)(2,1)S(1)} custom-call(f32[16,8,256]{2,1,0:T(8,128)} %sn_hbm.1, f32[16,8,256]{2,1,0:T(8,128)} %sb_hbm.1, f32[16,8,256]{2,1,0:T(8,128)} %rn_hbm.1, f32[16,8,256]{2,1,0:T(8,128)} %rb_hbm.1, f32[16,8,256]{2,1,0:T(8,128)} %speed_hbm.1, f32[16,8,256]{2,1,0:T(8,128)} %aniso_hbm.1, f32[16,8,256]{2,1,0:T(8,128)} %tilt_hbm.1, ...), custom_call_target="tpu_custom_call" | custom-call | tf_op jit(solution)/shard_map/pallas_call | solution.py:382
  38.5 0.7 %copy.16 = bf16[4,16,8,256]{3,2,1,0:T(8,128)(2,1)} copy(bf16[4,16,8,256]{3,2,1,0:T(8,128)(2,1)S(1)} %shard_map.136) | data formatting | bytes 524288

commit v2 on v1

--- a/solution.py
+++ b/solution.py
@@ -24,8 +24,8 @@
     lags_hbm, scells_hbm, swave_hbm, rcells_hbm, rtraces_hbm,
     out,
     pw, qv, speed, a1, a2, bins, wt, lags, scells, swave, rcells, rtraces, table, cache, inj, base, grad,
-    send0, send1, send2, recv0, recv1, recv2, win, acc,
-    in_sem, send_sem0, recv_sem0, send_sem1, recv_sem1, send_sem2, recv_sem2,
+    hw, share2, share1, send0, sendc, sendp, send1, send2, recv0, recvc, recvp, recv1, recv2, win, acc,
+    in_sem, send_sem0, recv_sem0, send_semc, recv_semc, send_semp, recv_semp, send_sem1, recv_sem1, send_sem2, recv_sem2,
 ):
     n = lax.axis_size("gy")
     me = lax.axis_index("gy")
@@ -50,25 +50,35 @@
         copy.start()
         copies[name] = copy
 
-    count = 0
-    for m, ref in enumerate((sn_hbm, rn_hbm)):
-        for x in range(halves):
-            fetch(("now", m, x), count, ref.at[:, :, pl.ds(x * LANES, LANES)], pw.at[0, m, x, inner, own, :])
-            count += 1
+    wanted = [
+        (("now", m, x), ref.at[:, :, pl.ds(x * LANES, LANES)], pw.at[0, m, x, inner, own, :])
+        for x in range(halves)
+        for m, ref in enumerate((sn_hbm, rn_hbm))
+    ]
+    wanted += [("rcells", rcells_hbm, rcells), ("rtraces", rtraces_hbm, rtraces)]
+    wanted += [("scells", scells_hbm, scells), ("swave", swave_hbm, swave)]
+    for name, ref, dst in (("speed", speed_hbm, speed), ("aniso", aniso_hbm, a1), ("tilt", tilt_hbm, a2)):
+        wanted += [((name, x), ref.at[:, :, pl.ds(x * LANES, LANES)], dst.at[x]) for x in range(halves)]
     for m, ref in enumerate((sb_hbm, rb_hbm)):
-        for x in range(halves):
-            fetch(("before", m, x), count, ref.at[:, :, pl.ds(x * LANES, LANES)], qv.at[m, x])
-            count += 1
-    for name, ref, dst in (("speed", speed_hbm, speed), ("aniso", aniso_hbm, a1), ("tilt", tilt_hbm, a2), ("bins", bins_hbm, bins)):
-        for x in range(halves):
-            fetch((name, x), count, ref.at[:, :, pl.ds(x * LANES, LANES)], dst.at[x])
-            count += 1
-    fetch("rcells", count, rcells_hbm, rcells)
-    fetch("rtraces", count + 1, rtraces_hbm, rtraces)
-    fetch("wt", count + 2, wt_hbm, wt)
-    fetch("lags", count + 3, lags_hbm, lags)
-    fetch("scells", count + 4, scells_hbm, scells)
-    fetch("swave", count + 5, swave_hbm, swave)
+        wanted += [(("before", m, x), ref.at[:, :, pl.ds(x * LANES, LANES)], qv.at[m, x]) for x in range(halves)]
+    wanted += [(("bins", x), bins_hbm.at[:, :, pl.ds(x * LANES, LANES)], bins.at[x]) for x in range(halves)]
+    wanted += [("wt", wt_hbm, wt), ("lags", lags_hbm, lags)]
+    for index, (name, src, dst) in enumerate(wanted):
+        fetch(name, index, src, dst)
+
+    edge = jnp.zeros((PAD, ROWS, LANES), F32)
+    plane = jnp.zeros((zs, ROWS, LANES), F32)
+    for x in range(halves):
+        for m in range(2):
+            for s in range(steps):
+                pw[s, m, x, pl.ds(0, PAD), own, :] = edge
+                pw[s, m, x, pl.ds(PAD + zs, PAD), own, :] = edge
+            pw[0, m, x, inner, pl.ds(0, ROWS), :] = plane
+            pw[0, m, x, inner, pl.ds(2 * ROWS, ROWS), :] = plane
+            hw[m, x, :, own, :] = plane
+            for padded in (grad, share1):
+                padded[m, x, pl.ds(0, PAD)] = edge
+                padded[m, x, pl.ds(PAD + zs, PAD)] = edge
 
     sub = lax.broadcasted_iota(jnp.int32, (ROWS, LANES), 0)
     lane = lax.broadcasted_iota(jnp.int32, (ROWS, LANES), 1)
@@ -102,24 +112,8 @@
         for copy in halo[x]:
             copy.start()
 
-    edge = jnp.zeros((PAD, ROWS, LANES), F32)
-    for x in range(halves):
-        for m in range(2):
-            for s in range(steps):
-                pw[s, m, x, pl.ds(0, PAD), own, :] = edge
-                pw[s, m, x, pl.ds(PAD + zs, PAD), own, :] = edge
-            grad[m, x, pl.ds(0, PAD)] = edge
-            grad[m, x, pl.ds(PAD + zs, PAD)] = edge
-
-    for x in range(halves):
-        copies[("speed", x)].wait()
-        copies[("aniso", x)].wait()
-        copies[("tilt", x)].wait()
-        a1[x] = speed[x] * (1.0 + 2.0 * a1[x])
-        a2[x] = speed[x] * a2[x]
-
     def local_part(step):
-        chunk = 2
+        chunk = 4
 
         def part(i, carry):
             z = i * chunk
@@ -198,54 +192,98 @@
 
     shift_bits = (halves * LANES).bit_length() - 1
 
-    def halo_rows(step, x, below, above):
-        low = below[...].astype(F32)
-        high = above[...].astype(F32)
-        pw[step, 0, x, inner, pl.ds(0, ROWS), :] = turn(low)
-        pw[step, 1, x, inner, pl.ds(0, ROWS), :] = low
-        pw[step, 0, x, inner, pl.ds(2 * ROWS, ROWS), :] = high
-        pw[step, 1, x, inner, pl.ds(2 * ROWS, ROWS), :] = turn(high)
-
-    def y_part(step, x, send):
-        chunk = 4
-
-        def along_y(i, carry):
-            z = i * chunk
+    def halo_rows(window, x, low, high):
+        window[0, x, :, pl.ds(0, ROWS), :] = turn(low)
+        window[1, x, :, pl.ds(0, ROWS), :] = low
+        window[0, x, :, pl.ds(2 * ROWS, ROWS), :] = high
+        window[1, x, :, pl.ds(2 * ROWS, ROWS), :] = turn(high)
+
+    part_chunk = 4
+
+    def along_y(window, x, whole):
+        def part(i, carry):
+            z = i * part_chunk
+            cells = pl.ds(z, part_chunk)
             for m in range(2):
 
                 def rows(k):
-                    return pw[step, m, x, pl.ds(PAD + z, chunk), pl.ds(ROWS + k, ROWS), :]
-
-                second = SECOND_COEF[0] * rows(0)
-                first = grad[m, x, pl.ds(PAD + z, chunk)]
+                    return window[m, x, cells, pl.ds(ROWS + k, ROWS), :]
+
+                second, first = 0.0, 0.0
+                if whole:
+                    second, first = SECOND_COEF[0] * rows(0), grad[m, x, pl.ds(PAD + z, part_chunk)]
                 for k in range(1, PAD + 1):
                     above, below = rows(k), rows(-k)
                     second = second + SECOND_COEF[k] * (above + below)
                     first = first + FIRST_COEF[k - 1] * (above - below)
-                grad[m, x, pl.ds(PAD + z, chunk)] = first
-                base[m, x, pl.ds(z, chunk)] = base[m, x, pl.ds(z, chunk)] + a1[x, pl.ds(z, chunk)] * second
+                grad[m, x, pl.ds(PAD + z, part_chunk)] = first
+                base[m, x, cells] = base[m, x, cells] + a1[x, cells] * second
             return carry
 
-        lax.fori_loop(0, zs // chunk, along_y, 0)
-
-        def finish(i, carry):
-            z = i * chunk
+        lax.fori_loop(0, zs // part_chunk, part, 0)
+
+    def along_z(padded, member, x, z):
+        mixed = jnp.zeros((part_chunk, ROWS, LANES), F32)
+        for k in range(1, PAD + 1):
+            mixed = mixed + FIRST_COEF[k - 1] * (
+                padded[member, x, pl.ds(PAD + z + k, part_chunk)] - padded[member, x, pl.ds(PAD + z - k, part_chunk)]
+            )
+        return mixed
+
+    def finish(step, x, send, whole=True):
+        def part(i, carry):
+            z = i * part_chunk
+            cells = pl.ds(z, part_chunk)
             new = []
             for m in range(2):
-                mixed = jnp.zeros((chunk, ROWS, LANES), F32)
-                for k in range(1, PAD + 1):
-                    mixed = mixed + FIRST_COEF[k - 1] * (
-                        grad[m, x, pl.ds(PAD + z + k, chunk)] - grad[m, x, pl.ds(PAD + z - k, chunk)]
-                    )
-                value = base[m, x, pl.ds(z, chunk)] + a2[x, pl.ds(z, chunk)] * mixed
+                value = base[m, x, cells] + a2[x, cells] * along_z(grad, m, x, z)
                 new.append(value)
+                if not whole:
+                    base[m, x, cells] = value
+                    continue
                 if step + 1 < steps:
-                    pw[step + 1, m, x, pl.ds(PAD + z, chunk), own, :] = value
-                win[step, m, x, pl.ds(z, chunk), pl.ds(2 * ROWS, ROWS), :] = value.astype(BF16).astype(F32)
-            pack(new[0], new[1], send, x, pl.ds(z, chunk))
+                    pw[step + 1, m, x, pl.ds(PAD + z, part_chunk), own, :] = value
+                win[step, m, x, cells, pl.ds(2 * ROWS, ROWS), :] = value.astype(BF16).astype(F32)
+            pack(new[0], new[1], send, x, cells)
             return carry
 
-        lax.fori_loop(0, zs // chunk, finish, 0)
+        lax.fori_loop(0, zs // part_chunk, part, 0)
+
+    def shares(x):
+        def part(i, carry):
+            z = i * part_chunk
+            for side in range(2):
+                second, first = [], []
+                for m in range(2):
+                    two, one = 0.0, 0.0
+                    for k in range(1, PAD + 1):
+                        row = ROWS - PAD + k if side == 0 else 2 * ROWS - k
+                        value = pw[0, m, x, pl.ds(PAD + z, part_chunk), pl.ds(row, ROWS), :]
+                        two = two + SECOND_COEF[k] * value
+                        one = one + (FIRST_COEF[k - 1] if side == 0 else -FIRST_COEF[k - 1]) * value
+                    second.append(two)
+                    first.append(one)
+                share2[side, x, pl.ds(z, part_chunk)] = jnp.where(low_rows, second[0], turn(second[1]))
+                share1[side, x, pl.ds(PAD + z, part_chunk)] = jnp.where(low_rows, first[0], turn(first[1]))
+            return carry
+
+        lax.fori_loop(0, zs // part_chunk, part, 0)
+
+    def border_rows(x):
+        whole = []
+        for side in range(2):
+            blocks = []
+            for z in range(0, zs, part_chunk):
+                cells = pl.ds(z, part_chunk)
+                pair = recvc[side, x, cells].astype(F32)
+                flat, tilted = jnp.where(low_rows, pair, turn(pair)), jnp.where(low_rows, turn(pair), pair)
+                blocks.append(
+                    recvp[x, side, cells].astype(F32)
+                    + flat * share2[side, x, cells]
+                    + tilted * along_z(share1, side, x, z)
+                )
+            whole.append(jnp.concatenate(blocks, axis=0))
+        halo_rows(pw.at[1, :, :, inner], x, whole[0], whole[1])
 
     def open_block(step, x, d, recv):
         slot = OFFSETS.index(d)
@@ -289,11 +327,38 @@
 
         lax.fori_loop(0, groups, part, 0)
 
+    injections()
+    for x in range(halves):
+        copies[("speed", x)].wait()
+        copies[("aniso", x)].wait()
+        copies[("tilt", x)].wait()
+        a1[x] = speed[x] * (1.0 + 2.0 * a1[x])
+        a2[x] = speed[x] * a2[x]
+        pack(a1[x], a2[x], sendc, x, pl.ds(0, zs))
+    coefs = [
+        remote(sendc.at[:, half], recvc.at[i], send_semc.at[i], recv_semc.at[i], d)
+        for i, (half, d) in enumerate(((HI, 1), (LO, -1)))
+    ]
+    for copy in coefs:
+        copy.start()
     for m in range(2):
         for x in range(halves):
             copies[("before", m, x)].wait()
-    injections()
     local_part(0)
+    partial = []
+    for x in range(halves):
+        along_y(pw.at[0, :, :, inner], x, True)
+        finish(0, x, sendp, whole=False)
+        partial.append(
+            [
+                remote(sendp.at[x, half], recvp.at[x, i], send_semp.at[2 * x + i], recv_semp.at[2 * x + i], d)
+                for i, (half, d) in enumerate(((HI, 1), (LO, -1)))
+            ]
+        )
+        for copy in partial[x]:
+            copy.start()
+    for x in range(halves):
+        shares(x)
     copies["wt"].wait()
     copies["lags"].wait()
     by_bin = [wt[b].astype(F32) for b in range(n_bin)]
@@ -305,37 +370,28 @@
         copies[("bins", x)].wait()
 
     slot_of = {d: OFFSETS.index(-d) for d in OFFSETS}
-    border = []
     for x in range(halves):
         for copy in halo[x]:
             copy.wait_recv()
-        halo_rows(0, x, recv0.at[x, 0], recv0.at[x, 1])
-        y_part(0, x, send1)
-        border.append(
-            [
-                remote(send1.at[x, half], recv1.at[slot_of[d], x, half], send_sem1.at[2 * x + i], recv_sem1.at[2 * x + i], d)
-                for i, (half, d) in enumerate(((HI, 1), (LO, -1)))
-            ]
-        )
-        for copy in border[x]:
-            copy.start()
+        halo_rows(hw, x, recv0[x, 0].astype(F32), recv0[x, 1].astype(F32))
+        along_y(hw, x, False)
+        finish(0, x, send1)
     rest = [
-        remote(send1.at[:, half], recv1.at[slot_of[d], :, half], send_sem1.at[2 * halves + i], recv_sem1.at[2 * halves + i], d)
-        for i, (half, d) in enumerate(((LO, 1), (HI, -1)))
-    ] + [
-        remote(send1, recv1.at[slot_of[d]], send_sem1.at[2 * halves + 2 + i], recv_sem1.at[2 * halves + 2 + i], d)
-        for i, d in enumerate((2, -2))
+        remote(send1, recv1.at[slot_of[d]], send_sem1.at[i], recv_sem1.at[i], d) for i, d in enumerate((2, -2, 1, -1))
     ]
     for copy in rest:
         copy.start()
 
     local_part(1)
+    for copy in coefs:
+        copy.wait_recv()
     final = []
     for x in range(halves):
-        for copy in border[x]:
+        for copy in partial[x]:
             copy.wait_recv()
-        halo_rows(1, x, recv1.at[slot_of[1], x, HI], recv1.at[slot_of[-1], x, LO])
-        y_part(1, x, send2)
+        border_rows(x)
+        along_y(pw.at[1, :, :, inner], x, True)
+        finish(1, x, send2)
         final.append(
             [
                 remote(send2.at[x], recv2.at[slot_of[d], x], send_sem2.at[4 * x + i], recv_sem2.at[4 * x + i], d)
@@ -359,7 +415,7 @@
             open_block(1, x, d, recv2)
         image(1, x)
 
-    for copy in sum([list(c) for c in halo + border + final], []) + rest:
+    for copy in sum([list(c) for c in halo + partial + final], []) + coefs + rest:
         copy.wait_send()
 
 
@@ -402,9 +458,16 @@
             pltpu.VMEM((steps, 2, halves, ROWS, LANES), F32),
             pltpu.VMEM((2,) + half, F32),
             pltpu.VMEM((2, halves, zs + 2 * PAD, ROWS, LANES), F32),
-            pltpu.VMEM(block, BF16),
-            pltpu.VMEM(block, BF16),
-            pltpu.VMEM(block, BF16),
+            pltpu.VMEM((2, halves, zs, 3 * ROWS, LANES), F32),
+            pltpu.VMEM((2,) + half, F32),
+            pltpu.VMEM((2, halves, zs + 2 * PAD, ROWS, LANES), F32),
+            pltpu.VMEM(block, BF16),
+            pltpu.VMEM(block, BF16),
+            pltpu.VMEM(block, BF16),
+            pltpu.VMEM(block, BF16),
+            pltpu.VMEM(block, BF16),
+            pltpu.VMEM(block, BF16),
+            pltpu.VMEM((2,) + half, BF16),
             pltpu.VMEM(block, BF16),
             pltpu.VMEM((len(OFFSETS),) + block, BF16),
             pltpu.VMEM((len(OFFSETS),) + block, BF16),
@@ -413,8 +476,12 @@
             dma((8 * halves + 6,)),
             dma((2 * halves,)),
             dma((2 * halves,)),
-            dma((2 * halves + 4,)),
-            dma((2 * halves + 4,)),
+            dma((2,)),
+            dma((2,)),
+            dma((2 * halves,)),
+            dma((2 * halves,)),
+            dma((4,)),
+            dma((4,)),
             dma((4 * halves,)),
             dma((4 * halves,)),
         ],

time: 39.3 us -> 39.3 us (level)
  no operation moved by 1% of the time
where the time goes in v2:
time: 39.3 us; the launch traced here: 39.1 us
  Pallas kernels  38.4 us (98%)
  local copies, waits for them, and re-layouts  0.71 us (2%)
    pallas_call x1, Pallas kernels, per_device(): pl.pallas_call(kernel, out_shape=pltpu.VMEM((n_ang, zs, rows, width), BF1...  38.4 us

profile of v2, /device:TPU:513, one launch (start us, length us, event | category | flops | bytes accessed | tf_op | source)
XLA Modules:
  0.0 39.1 jit_solution(3555140559080157512)
XLA Ops:
  0.0 38.4 %shard_map.136 = bf16[4,16,8,256]{3,2,1,0:T(8,128)(2,1)S(1)} custom-call(f32[16,8,256]{2,1,0:T(8,128)} %sn_hbm.1, f32[16,8,256]{2,1,0:T(8,128)} %sb_hbm.1, f32[16,8,256]{2,1,0:T(8,128)} %rn_hbm.1, f32[16,8,256]{2,1,0:T(8,128)} %rb_hbm.1, f32[16,8,256]{2,1,0:T(8,128)} %speed_hbm.1, f32[16,8,256]{2,1,0:T(8,128)} %aniso_hbm.1, f32[16,8,256]{2,1,0:T(8,128)} %tilt_hbm.1, ...), custom_call_target="tpu_custom_call" | custom-call | tf_op jit(solution)/shard_map/pallas_call | solution.py:438
  38.4 0.7 %copy.16 = bf16[4,16,8,256]{3,2,1,0:T(8,128)(2,1)} copy(bf16[4,16,8,256]{3,2,1,0:T(8,128)(2,1)S(1)} %shard_map.136) | data formatting | bytes 524288

commit v3 on v2

--- a/solution.py
+++ b/solution.py
@@ -17,6 +17,8 @@
 PAD = 4
 LO, HI = 0, 1
 OFFSETS = (-2, -1, 1, 2)
+PARTNER, OUTER, FAR, PASSED = range(4)
+PIECES = 2
 
 
 def kernel(
@@ -30,6 +32,19 @@
     n = lax.axis_size("gy")
     me = lax.axis_index("gy")
     peer = {d: lax.rem(me + (d + n), n) for d in OFFSETS}
+    side_of = 1 - 2 * lax.rem(me, 2)
+    target = {
+        PARTNER: lax.rem(me + side_of + n, n),
+        OUTER: lax.rem(me - side_of + n, n),
+        FAR: lax.rem(me + 2 * side_of + n, n),
+    }
+    target[PASSED] = target[PARTNER]
+    block_row = {
+        PARTNER: (2 + side_of) * ROWS,
+        OUTER: (2 - side_of) * ROWS,
+        FAR: (2 - 2 * side_of) * ROWS,
+        PASSED: (2 + 2 * side_of) * ROWS,
+    }
     zs = sn_hbm.shape[0]
     halves = sn_hbm.shape[2] // LANES
     n_bin, n_ang, n_off = wt_hbm.shape
@@ -50,13 +65,13 @@
         copy.start()
         copies[name] = copy
 
-    wanted = [
+    wanted = [("rcells", rcells_hbm, rcells), ("rtraces", rtraces_hbm, rtraces)]
+    wanted += [("scells", scells_hbm, scells), ("swave", swave_hbm, swave)]
+    wanted += [
         (("now", m, x), ref.at[:, :, pl.ds(x * LANES, LANES)], pw.at[0, m, x, inner, own, :])
         for x in range(halves)
         for m, ref in enumerate((sn_hbm, rn_hbm))
     ]
-    wanted += [("rcells", rcells_hbm, rcells), ("rtraces", rtraces_hbm, rtraces)]
-    wanted += [("scells", scells_hbm, scells), ("swave", swave_hbm, swave)]
     for name, ref, dst in (("speed", speed_hbm, speed), ("aniso", aniso_hbm, a1), ("tilt", tilt_hbm, a2)):
         wanted += [((name, x), ref.at[:, :, pl.ds(x * LANES, LANES)], dst.at[x]) for x in range(halves)]
     for m, ref in enumerate((sb_hbm, rb_hbm)):
@@ -91,65 +106,12 @@
         send[x, LO, where_z] = jnp.where(low_rows, source, turn(receiver)).astype(BF16)
         send[x, HI, where_z] = jnp.where(low_rows, turn(source), receiver).astype(BF16)
 
-    def remote(src, dst, ssem, rsem, d):
+    def remote(src, dst, ssem, rsem, device):
         return pltpu.make_async_remote_copy(
-            src_ref=src, dst_ref=dst, send_sem=ssem, recv_sem=rsem, device_id={"gy": peer[d]}, device_id_type=MESH
+            src_ref=src, dst_ref=dst, send_sem=ssem, recv_sem=rsem, device_id={"gy": device}, device_id_type=MESH
         )
 
-    halo = [
-        (
-            remote(send0.at[x, HI], recv0.at[x, 0], send_sem0.at[2 * x], recv_sem0.at[2 * x], 1),
-            remote(send0.at[x, LO], recv0.at[x, 1], send_sem0.at[2 * x + 1], recv_sem0.at[2 * x + 1], -1),
-        )
-        for x in range(halves)
-    ]
-    for x in range(halves):
-        for m in range(2):
-            copies[("now", m, x)].wait()
-        pack(pw[0, 0, x, inner, own, :], pw[0, 1, x, inner, own, :], send0, x, pl.ds(0, zs))
-        if x == 0:
-            pl.semaphore_wait(barrier, len(OFFSETS))
-        for copy in halo[x]:
-            copy.start()
-
-    def local_part(step):
-        chunk = 4
-
-        def part(i, carry):
-            z = i * chunk
-            for m in range(2):
-                f = [pw[step, m, x, pl.ds(PAD + z, chunk), own, :] for x in range(halves)]
-                first = [jnp.zeros_like(v) for v in f]
-                second = [SECOND_COEF[0] * v for v in f]
-                for k in range(1, PAD + 1):
-                    up = [pltpu.roll(v, LANES - k, axis=2) for v in f] + [jnp.zeros_like(f[0])]
-                    down = [jnp.zeros_like(f[0])] + [pltpu.roll(v, k, axis=2) for v in f]
-                    for x in range(halves):
-                        above = jnp.where(lane < LANES - k, up[x], up[x + 1])
-                        below = jnp.where(lane >= k, down[x + 1], down[x])
-                        second[x] = second[x] + SECOND_COEF[k] * (above + below)
-                        first[x] = first[x] + FIRST_COEF[k - 1] * (above - below)
-                for x in range(halves):
-                    grad[m, x, pl.ds(PAD + z, chunk)] = first[x]
-                    along_z = SECOND_COEF[0] * f[x]
-                    for k in range(1, PAD + 1):
-                        along_z = along_z + SECOND_COEF[k] * (
-                            pw[step, m, x, pl.ds(PAD + z + k, chunk), own, :]
-                            + pw[step, m, x, pl.ds(PAD + z - k, chunk), own, :]
-                        )
-                    before = qv[m, x, pl.ds(z, chunk)] if step == 0 else pw[step - 1, m, x, pl.ds(PAD + z, chunk), own, :]
-                    base[m, x, pl.ds(z, chunk)] = (
-                        2.0 * f[x]
-                        - before
-                        + a1[x, pl.ds(z, chunk)] * second[x]
-                        + speed[x, pl.ds(z, chunk)] * along_z
-                    )
-            return carry
-
-        lax.fori_loop(0, zs // chunk, part, 0)
-        for m in range(2):
-            for x in range(halves):
-                base[m, x, 0] = base[m, x, 0] + inj[step, m, x]
+    shift_bits = (halves * LANES).bit_length() - 1
 
     def injections():
         first_row = me * ROWS
@@ -190,7 +152,62 @@
                     total = total + jnp.where((sub == row) & (lane == col), swave[s, i], 0.0)
                 inj[s, 0, x] = total
 
-    shift_bits = (halves * LANES).bit_length() - 1
+    injections()
+
+    halo = [
+        (
+            remote(send0.at[x, HI], recv0.at[x, 0], send_sem0.at[2 * x], recv_sem0.at[2 * x], peer[1]),
+            remote(send0.at[x, LO], recv0.at[x, 1], send_sem0.at[2 * x + 1], recv_sem0.at[2 * x + 1], peer[-1]),
+        )
+        for x in range(halves)
+    ]
+    for x in range(halves):
+        for m in range(2):
+            copies[("now", m, x)].wait()
+        pack(pw[0, 0, x, inner, own, :], pw[0, 1, x, inner, own, :], send0, x, pl.ds(0, zs))
+        if x == 0:
+            pl.semaphore_wait(barrier, len(OFFSETS))
+        for copy in halo[x]:
+            copy.start()
+
+    def local_part(step):
+        chunk = 4
+
+        def part(i, carry):
+            z = i * chunk
+            for m in range(2):
+                f = [pw[step, m, x, pl.ds(PAD + z, chunk), own, :] for x in range(halves)]
+                first = [jnp.zeros_like(v) for v in f]
+                second = [SECOND_COEF[0] * v for v in f]
+                for k in range(1, PAD + 1):
+                    up = [pltpu.roll(v, LANES - k, axis=2) for v in f] + [jnp.zeros_like(f[0])]
+                    down = [jnp.zeros_like(f[0])] + [pltpu.roll(v, k, axis=2) for v in f]
+                    for x in range(halves):
+                        above = jnp.where(lane < LANES - k, up[x], up[x + 1])
+                        below = jnp.where(lane >= k, down[x + 1], down[x])
+                        second[x] = second[x] + SECOND_COEF[k] * (above + below)
+                        first[x] = first[x] + FIRST_COEF[k - 1] * (above - below)
+                for x in range(halves):
+                    grad[m, x, pl.ds(PAD + z, chunk)] = first[x]
+                    along_z = SECOND_COEF[0] * f[x]
+                    for k in range(1, PAD + 1):
+                        along_z = along_z + SECOND_COEF[k] * (
+                            pw[step, m, x, pl.ds(PAD + z + k, chunk), own, :]
+                            + pw[step, m, x, pl.ds(PAD + z - k, chunk), own, :]
+                        )
+                    before = qv[m, x, pl.ds(z, chunk)] if step == 0 else pw[step - 1, m, x, pl.ds(PAD + z, chunk), own, :]
+                    base[m, x, pl.ds(z, chunk)] = (
+                        2.0 * f[x]
+                        - before
+                        + a1[x, pl.ds(z, chunk)] * second[x]
+                        + speed[x, pl.ds(z, chunk)] * along_z
+                    )
+            return carry
+
+        lax.fori_loop(0, zs // chunk, part, 0)
+        for m in range(2):
+            for x in range(halves):
+                base[m, x, 0] = base[m, x, 0] + inj[step, m, x]
 
     def halo_rows(window, x, low, high):
         window[0, x, :, pl.ds(0, ROWS), :] = turn(low)
@@ -285,20 +302,19 @@
             whole.append(jnp.concatenate(blocks, axis=0))
         halo_rows(pw.at[1, :, :, inner], x, whole[0], whole[1])
 
-    def open_block(step, x, d, recv):
-        slot = OFFSETS.index(d)
-        rows = pl.ds((2 + d) * ROWS, ROWS)
-        low = recv[slot, x, LO].astype(F32)
-        high = recv[slot, x, HI].astype(F32)
-        win[step, 0, x, :, rows, :] = jnp.where(low_rows, low, turn(high))
-        win[step, 1, x, :, rows, :] = jnp.where(low_rows, turn(low), high)
+    def open_block(step, role, recv, x, z, length):
+        cells = pl.ds(z, length)
+        rows = pl.ds(pl.multiple_of(block_row[role], ROWS), ROWS)
+        low = recv[role, x, LO, cells].astype(F32)
+        high = recv[role, x, HI, cells].astype(F32)
+        win[step, 0, x, cells, rows, :] = jnp.where(low_rows, low, turn(high))
+        win[step, 1, x, cells, rows, :] = jnp.where(low_rows, turn(low), high)
 
     chunk = 4
-    groups = zs // chunk
-
-    def image(step, x):
+
+    def image(step, x, start, length):
         def part(i, carry):
-            z = i * chunk
+            z = start + i * chunk
             if step == 0:
                 bin_ids = [bins[x, z + j] for j in range(chunk)]
                 total = [jnp.zeros((chunk, ROWS, LANES), F32)] * n_ang
@@ -325,9 +341,8 @@
                     acc[a, x, pl.ds(z, chunk)] = total[a]
             return carry
 
-        lax.fori_loop(0, groups, part, 0)
-
-    injections()
+        lax.fori_loop(0, length // chunk, part, 0)
+
     for x in range(halves):
         copies[("speed", x)].wait()
         copies[("aniso", x)].wait()
@@ -336,7 +351,7 @@
         a2[x] = speed[x] * a2[x]
         pack(a1[x], a2[x], sendc, x, pl.ds(0, zs))
     coefs = [
-        remote(sendc.at[:, half], recvc.at[i], send_semc.at[i], recv_semc.at[i], d)
+        remote(sendc.at[:, half], recvc.at[i], send_semc.at[i], recv_semc.at[i], peer[d])
         for i, (half, d) in enumerate(((HI, 1), (LO, -1)))
     ]
     for copy in coefs:
@@ -351,7 +366,7 @@
         finish(0, x, sendp, whole=False)
         partial.append(
             [
-                remote(sendp.at[x, half], recvp.at[x, i], send_semp.at[2 * x + i], recv_semp.at[2 * x + i], d)
+                remote(sendp.at[x, half], recvp.at[x, i], send_semp.at[2 * x + i], recv_semp.at[2 * x + i], peer[d])
                 for i, (half, d) in enumerate(((HI, 1), (LO, -1)))
             ]
         )
@@ -369,53 +384,85 @@
     for x in range(halves):
         copies[("bins", x)].wait()
 
-    slot_of = {d: OFFSETS.index(-d) for d in OFFSETS}
     for x in range(halves):
         for copy in halo[x]:
             copy.wait_recv()
         halo_rows(hw, x, recv0[x, 0].astype(F32), recv0[x, 1].astype(F32))
         along_y(hw, x, False)
         finish(0, x, send1)
-    rest = [
-        remote(send1, recv1.at[slot_of[d]], send_sem1.at[i], recv_sem1.at[i], d) for i, d in enumerate((2, -2, 1, -1))
-    ]
-    for copy in rest:
-        copy.start()
+    first = {
+        role: remote(
+            recv1.at[OUTER] if role == PASSED else send1,
+            recv1.at[role],
+            send_sem1.at[role],
+            recv_sem1.at[role],
+            target[role],
+        )
+        for role in target
+    }
+    for role in (FAR, OUTER, PARTNER):
+        first[role].start()
 
     local_part(1)
     for copy in coefs:
         copy.wait_recv()
+    length = zs // PIECES
+    pieces = [(x, p * length) for x in range(halves) for p in range(PIECES)]
     final = []
+    for index, (x, z) in enumerate(pieces):
+        cells = (x, slice(None), pl.ds(z, length))
+        final.append(
+            {
+                role: remote(
+                    recv2.at[(OUTER,) + cells] if role == PASSED else send2.at[cells],
+                    recv2.at[(role,) + cells],
+                    send_sem2.at[4 * index + role],
+                    recv_sem2.at[4 * index + role],
+                    target[role],
+                )
+                for role in target
+            }
+        )
     for x in range(halves):
         for copy in partial[x]:
             copy.wait_recv()
         border_rows(x)
         along_y(pw.at[1, :, :, inner], x, True)
         finish(1, x, send2)
-        final.append(
-            [
-                remote(send2.at[x], recv2.at[slot_of[d], x], send_sem2.at[4 * x + i], recv_sem2.at[4 * x + i], d)
-                for i, d in enumerate((2, -2, 1, -1))
-            ]
-        )
-        for copy in final[x]:
-            copy.start()
-
-    for copy in rest:
-        copy.wait_recv()
-    for x in range(halves):
-        for d in OFFSETS:
-            open_block(0, x, d, recv1)
-        image(0, x)
-
-    for x in range(halves):
-        for copy in final[x]:
-            copy.wait_recv()
-        for d in OFFSETS:
-            open_block(1, x, d, recv2)
-        image(1, x)
-
-    for copy in sum([list(c) for c in halo + partial + final], []) + coefs + rest:
+        for index, (x_of, z) in enumerate(pieces):
+            if x_of == x:
+                for role in (FAR, OUTER, PARTNER):
+                    final[index][role].start()
+
+    first[OUTER].wait_recv()
+    first[PASSED].start()
+    for role in (OUTER, PARTNER, FAR, PASSED):
+        if role != OUTER:
+            first[role].wait_recv()
+        for x in range(halves):
+            open_block(0, role, recv1, x, 0, zs)
+    for x in range(halves):
+        image(0, x, 0, zs)
+
+    def last_image(index):
+        x, z = pieces[index]
+        final[index][PASSED].wait_recv()
+        open_block(1, PASSED, recv2, x, z, length)
+        image(1, x, z, length)
+
+    for index, (x, z) in enumerate(pieces):
+        final[index][OUTER].wait_recv()
+        final[index][PASSED].start()
+        for role in (OUTER, PARTNER, FAR):
+            if role != OUTER:
+                final[index][role].wait_recv()
+            open_block(1, role, recv2, x, z, length)
+        if index:
+            last_image(index - 1)
+    last_image(len(pieces) - 1)
+
+    sent = coefs + list(first.values()) + sum([list(c) for c in halo + partial], [])
+    for copy in sent + sum([list(c.values()) for c in final], []):
         copy.wait_send()
 
 
@@ -469,8 +516,8 @@
             pltpu.VMEM(block, BF16),
             pltpu.VMEM((2,) + half, BF16),
             pltpu.VMEM(block, BF16),
-            pltpu.VMEM((len(OFFSETS),) + block, BF16),
-            pltpu.VMEM((len(OFFSETS),) + block, BF16),
+            pltpu.VMEM((4,) + block, BF16),
+            pltpu.VMEM((4,) + block, BF16),
             pltpu.VMEM((steps, 2, halves, zs, 5 * ROWS, LANES), F32),
             pltpu.VMEM((n_ang,) + half, F32),
             dma((8 * halves + 6,)),
@@ -482,8 +529,8 @@
             dma((2 * halves,)),
             dma((4,)),
             dma((4,)),
-            dma((4 * halves,)),
-            dma((4 * halves,)),
+            dma((4 * halves * PIECES,)),
+            dma((4 * halves * PIECES,)),
         ],
         compiler_params=pltpu.CompilerParams(collective_id=0, has_side_effects=True),
     )(

time: 39.3 us -> 40.5 us (1.031)
  Pallas kernels: 38.4 us -> 39.6 us
    pallas_call x1, Pallas kernels: 38.4 us -> 39.6 us  [per_device(): pl.pallas_call(kernel, out_shape=pltpu.VMEM((n_ang, zs, rows, width), BF1...]
where the time goes in v3:
time: 40.5 us; the launch traced here: 40.3 us
  Pallas kernels  39.6 us (98%)
  local copies, waits for them, and re-layouts  0.71 us (2%)
    pallas_call x1, Pallas kernels, per_device(): pl.pallas_call(kernel, out_shape=pltpu.VMEM((n_ang, zs, rows, width), BF1...  39.6 us

profile of v3, /device:TPU:513, one launch (start us, length us, event | category | flops | bytes accessed | tf_op | source)
XLA Modules:
  0.0 40.3 jit_solution(14057935315721694892)
XLA Ops:
  0.0 39.6 %shard_map.136 = bf16[4,16,8,256]{3,2,1,0:T(8,128)(2,1)S(1)} custom-call(f32[16,8,256]{2,1,0:T(8,128)} %sn_hbm.1, f32[16,8,256]{2,1,0:T(8,128)} %sb_hbm.1, f32[16,8,256]{2,1,0:T(8,128)} %rn_hbm.1, f32[16,8,256]{2,1,0:T(8,128)} %rb_hbm.1, f32[16,8,256]{2,1,0:T(8,128)} %speed_hbm.1, f32[16,8,256]{2,1,0:T(8,128)} %aniso_hbm.1, f32[16,8,256]{2,1,0:T(8,128)} %tilt_hbm.1, ...), custom_call_target="tpu_custom_call" | custom-call | tf_op jit(solution)/shard_map/pallas_call | solution.py:485
  39.6 0.7 %copy.16 = bf16[4,16,8,256]{3,2,1,0:T(8,128)(2,1)} copy(bf16[4,16,8,256]{3,2,1,0:T(8,128)(2,1)S(1)} %shard_map.136) | data formatting | bytes 524288

commit v4 on v3

--- a/solution.py
+++ b/solution.py
@@ -17,7 +17,8 @@
 PAD = 4
 LO, HI = 0, 1
 OFFSETS = (-2, -1, 1, 2)
-PARTNER, OUTER, FAR, PASSED = range(4)
+DIRECT = ((2, -1, 1), (2, -2, -1))
+PASSED = ((1, 2), (-2, -1))
 PIECES = 2
 
 
@@ -32,19 +33,7 @@
     n = lax.axis_size("gy")
     me = lax.axis_index("gy")
     peer = {d: lax.rem(me + (d + n), n) for d in OFFSETS}
-    side_of = 1 - 2 * lax.rem(me, 2)
-    target = {
-        PARTNER: lax.rem(me + side_of + n, n),
-        OUTER: lax.rem(me - side_of + n, n),
-        FAR: lax.rem(me + 2 * side_of + n, n),
-    }
-    target[PASSED] = target[PARTNER]
-    block_row = {
-        PARTNER: (2 + side_of) * ROWS,
-        OUTER: (2 - side_of) * ROWS,
-        FAR: (2 - 2 * side_of) * ROWS,
-        PASSED: (2 + 2 * side_of) * ROWS,
-    }
+    odd = lax.rem(me, 2) == 1
     zs = sn_hbm.shape[0]
     halves = sn_hbm.shape[2] // LANES
     n_bin, n_ang, n_off = wt_hbm.shape
@@ -65,13 +54,13 @@
         copy.start()
         copies[name] = copy
 
-    wanted = [("rcells", rcells_hbm, rcells), ("rtraces", rtraces_hbm, rtraces)]
-    wanted += [("scells", scells_hbm, scells), ("swave", swave_hbm, swave)]
-    wanted += [
+    wanted = [
         (("now", m, x), ref.at[:, :, pl.ds(x * LANES, LANES)], pw.at[0, m, x, inner, own, :])
         for x in range(halves)
         for m, ref in enumerate((sn_hbm, rn_hbm))
     ]
+    wanted += [("rcells", rcells_hbm, rcells), ("rtraces", rtraces_hbm, rtraces)]
+    wanted += [("scells", scells_hbm, scells), ("swave", swave_hbm, swave)]
     for name, ref, dst in (("speed", speed_hbm, speed), ("aniso", aniso_hbm, a1), ("tilt", tilt_hbm, a2)):
         wanted += [((name, x), ref.at[:, :, pl.ds(x * LANES, LANES)], dst.at[x]) for x in range(halves)]
     for m, ref in enumerate((sb_hbm, rb_hbm)):
@@ -152,8 +141,6 @@
                     total = total + jnp.where((sub == row) & (lane == col), swave[s, i], 0.0)
                 inj[s, 0, x] = total
 
-    injections()
-
     halo = [
         (
             remote(send0.at[x, HI], recv0.at[x, 0], send_sem0.at[2 * x], recv_sem0.at[2 * x], peer[1]),
@@ -302,11 +289,12 @@
             whole.append(jnp.concatenate(blocks, axis=0))
         halo_rows(pw.at[1, :, :, inner], x, whole[0], whole[1])
 
-    def open_block(step, role, recv, x, z, length):
+    def open_block(step, d, recv, x, z, length):
         cells = pl.ds(z, length)
-        rows = pl.ds(pl.multiple_of(block_row[role], ROWS), ROWS)
-        low = recv[role, x, LO, cells].astype(F32)
-        high = recv[role, x, HI, cells].astype(F32)
+        rows = pl.ds((2 + d) * ROWS, ROWS)
+        slot = OFFSETS.index(d)
+        low = recv[slot, x, LO, cells].astype(F32)
+        high = recv[slot, x, HI, cells].astype(F32)
         win[step, 0, x, cells, rows, :] = jnp.where(low_rows, low, turn(high))
         win[step, 1, x, cells, rows, :] = jnp.where(low_rows, turn(low), high)
 
@@ -343,6 +331,7 @@
 
         lax.fori_loop(0, length // chunk, part, 0)
 
+    injections()
     for x in range(halves):
         copies[("speed", x)].wait()
         copies[("aniso", x)].wait()
@@ -390,39 +379,57 @@
         halo_rows(hw, x, recv0[x, 0].astype(F32), recv0[x, 1].astype(F32))
         along_y(hw, x, False)
         finish(0, x, send1)
-    first = {
-        role: remote(
-            recv1.at[OUTER] if role == PASSED else send1,
-            recv1.at[role],
-            send_sem1.at[role],
-            recv_sem1.at[role],
-            target[role],
-        )
-        for role in target
-    }
-    for role in (FAR, OUTER, PARTNER):
-        first[role].start()
+    def direct(send, recv, send_sems, recv_sems, cells):
+        for parity, here in enumerate((jnp.logical_not(odd), odd)):
+
+            @pl.when(here)
+            def _():
+                for i, d in enumerate(DIRECT[parity]):
+                    slot = OFFSETS.index(-d)
+                    remote(send.at[cells], recv.at[(slot,) + cells], send_sems[i], recv_sems[slot], peer[d]).start()
+
+    def passed(recv, send_sems, recv_sems, cells, index):
+        here, there = (OFFSETS.index(d) for d in PASSED[index])
+        return remote(recv.at[(here,) + cells], recv.at[(there,) + cells], send_sems[index], recv_sems[there], peer[-1])
+
+    def collect(step, recv, send_sems, recv_sems, cells, x_list, z, length):
+        for d in (1, -2, -1, 2):
+            slot = OFFSETS.index(d)
+            remote(recv.at[(slot,) + cells], recv.at[(slot,) + cells], send_sems[0], recv_sems[slot], peer[1]).wait_recv()
+            for index, (source, _) in enumerate(PASSED):
+                if source == d:
+
+                    @pl.when(odd)
+                    def _():
+                        passed(recv, send_sems[3:], recv_sems, cells, index).start()
+
+        for d in OFFSETS:
+            for x in x_list:
+                open_block(step, d, recv, x, z, length)
+
+    def sent(send, recv, send_sems, recv_sems, cells):
+        for i in range(3):
+            remote(send.at[cells], recv.at[(0,) + cells], send_sems[i], recv_sems[0], peer[1]).wait_send()
+
+        @pl.when(odd)
+        def _():
+            for index in range(len(PASSED)):
+                passed(recv, send_sems[3:], recv_sems, cells, index).wait_send()
+
+    everything = (pl.ds(0, halves),)
+    first_sems = [send_sem1.at[i] for i in range(5)], [recv_sem1.at[i] for i in range(4)]
+    direct(send1, recv1, *first_sems, everything)
 
     local_part(1)
     for copy in coefs:
         copy.wait_recv()
     length = zs // PIECES
     pieces = [(x, p * length) for x in range(halves) for p in range(PIECES)]
-    final = []
-    for index, (x, z) in enumerate(pieces):
-        cells = (x, slice(None), pl.ds(z, length))
-        final.append(
-            {
-                role: remote(
-                    recv2.at[(OUTER,) + cells] if role == PASSED else send2.at[cells],
-                    recv2.at[(role,) + cells],
-                    send_sem2.at[4 * index + role],
-                    recv_sem2.at[4 * index + role],
-                    target[role],
-                )
-                for role in target
-            }
-        )
+    cells_of = [(x, slice(None), pl.ds(z, length)) for x, z in pieces]
+    last_sems = [
+        ([send_sem2.at[5 * index + i] for i in range(5)], [recv_sem2.at[4 * index + i] for i in range(4)])
+        for index in range(len(pieces))
+    ]
     for x in range(halves):
         for copy in partial[x]:
             copy.wait_recv()
@@ -431,39 +438,20 @@
         finish(1, x, send2)
         for index, (x_of, z) in enumerate(pieces):
             if x_of == x:
-                for role in (FAR, OUTER, PARTNER):
-                    final[index][role].start()
-
-    first[OUTER].wait_recv()
-    first[PASSED].start()
-    for role in (OUTER, PARTNER, FAR, PASSED):
-        if role != OUTER:
-            first[role].wait_recv()
-        for x in range(halves):
-            open_block(0, role, recv1, x, 0, zs)
+                direct(send2, recv2, *last_sems[index], cells_of[index])
+
+    collect(0, recv1, *first_sems, everything, range(halves), 0, zs)
     for x in range(halves):
         image(0, x, 0, zs)
-
-    def last_image(index):
-        x, z = pieces[index]
-        final[index][PASSED].wait_recv()
-        open_block(1, PASSED, recv2, x, z, length)
+    for index, (x, z) in enumerate(pieces):
+        collect(1, recv2, *last_sems[index], cells_of[index], (x,), z, length)
         image(1, x, z, length)
 
-    for index, (x, z) in enumerate(pieces):
-        final[index][OUTER].wait_recv()
-        final[index][PASSED].start()
-        for role in (OUTER, PARTNER, FAR):
-            if role != OUTER:
-                final[index][role].wait_recv()
-            open_block(1, role, recv2, x, z, length)
-        if index:
-            last_image(index - 1)
-    last_image(len(pieces) - 1)
-
-    sent = coefs + list(first.values()) + sum([list(c) for c in halo + partial], [])
-    for copy in sent + sum([list(c.values()) for c in final], []):
+    for copy in coefs + sum([list(c) for c in halo + partial], []):
         copy.wait_send()
+    sent(send1, recv1, *first_sems, everything)
+    for index in range(len(pieces)):
+        sent(send2, recv2, *last_sems[index], cells_of[index])
 
 
 def per_device(
@@ -527,9 +515,9 @@
             dma((2,)),
             dma((2 * halves,)),
             dma((2 * halves,)),
+            dma((5,)),
             dma((4,)),
-            dma((4,)),
-            dma((4 * halves * PIECES,)),
+            dma((5 * halves * PIECES,)),
             dma((4 * halves * PIECES,)),
         ],
         compiler_params=pltpu.CompilerParams(collective_id=0, has_side_effects=True),

time: 40.5 us -> 37.5 us (0.926)
  Pallas kernels: 39.6 us -> 36.7 us
    pallas_call x1, Pallas kernels: 39.6 us -> 36.7 us  [per_device(): pl.pallas_call(kernel, out_shape=pltpu.VMEM((n_ang, zs, rows, width), BF1...]
where the time goes in v4:
time: 37.5 us; the launch traced here: 37.4 us
  Pallas kernels  36.7 us (98%)
  local copies, waits for them, and re-layouts  0.71 us (2%)
    pallas_call x1, Pallas kernels, per_device(): pl.pallas_call(kernel, out_shape=pltpu.VMEM((n_ang, zs, rows, width), BF1...  36.7 us

profile of v4, /device:TPU:513, one launch (start us, length us, event | category | flops | bytes accessed | tf_op | source)
XLA Modules:
  0.0 37.4 jit_solution(7353411748473580987)
XLA Ops:
  0.0 36.7 %shard_map.136 = bf16[4,16,8,256]{3,2,1,0:T(8,128)(2,1)S(1)} custom-call(f32[16,8,256]{2,1,0:T(8,128)} %sn_hbm.1, f32[16,8,256]{2,1,0:T(8,128)} %sb_hbm.1, f32[16,8,256]{2,1,0:T(8,128)} %rn_hbm.1, f32[16,8,256]{2,1,0:T(8,128)} %rb_hbm.1, f32[16,8,256]{2,1,0:T(8,128)} %speed_hbm.1, f32[16,8,256]{2,1,0:T(8,128)} %aniso_hbm.1, f32[16,8,256]{2,1,0:T(8,128)} %tilt_hbm.1, ...), custom_call_target="tpu_custom_call" | custom-call | tf_op jit(solution)/shard_map/pallas_call | solution.py:473
  36.7 0.7 %copy.16 = bf16[4,16,8,256]{3,2,1,0:T(8,128)(2,1)} copy(bf16[4,16,8,256]{3,2,1,0:T(8,128)(2,1)S(1)} %shard_map.136) | data formatting | bytes 524288

commit v5 on v4

--- a/solution.py
+++ b/solution.py
@@ -19,6 +19,7 @@
 OFFSETS = (-2, -1, 1, 2)
 DIRECT = ((2, -1, 1), (2, -2, -1))
 PASSED = ((1, 2), (-2, -1))
+KEPT = 4
 PIECES = 2
 
 
@@ -27,7 +28,7 @@
     lags_hbm, scells_hbm, swave_hbm, rcells_hbm, rtraces_hbm,
     out,
     pw, qv, speed, a1, a2, bins, wt, lags, scells, swave, rcells, rtraces, table, cache, inj, base, grad,
-    hw, share2, share1, send0, sendc, sendp, send1, send2, recv0, recvc, recvp, recv1, recv2, win, acc,
+    hw, share2, share1, send0, sendc, sendp, send1, send2, recv0, recvc, recvp, recv1, recv2, win,
     in_sem, send_sem0, recv_sem0, send_semc, recv_semc, send_semp, recv_semp, send_sem1, recv_sem1, send_sem2, recv_sem2,
 ):
     n = lax.axis_size("gy")
@@ -37,6 +38,7 @@
     zs = sn_hbm.shape[0]
     halves = sn_hbm.shape[2] // LANES
     n_bin, n_ang, n_off = wt_hbm.shape
+    kept = cache.shape[1]
     steps = swave.shape[0]
     n_src = scells.shape[0]
     rec_rows = rcells_hbm.shape[0]
@@ -300,33 +302,39 @@
 
     chunk = 4
 
-    def image(step, x, start, length):
+    def gathered(h, a, bin_ids):
+        row = table[h, a]
+        return jnp.stack([jnp.take_along_axis(row, ids, axis=0) for ids in bin_ids])
+
+    def keep_weights(x):
+        def part(i, carry):
+            z = i * chunk
+            bin_ids = [bins[x, z + j] for j in range(chunk)]
+            for h in range(n_off):
+                for a in range(kept):
+                    cache[h, a, x, pl.ds(z, chunk)] = gathered(h, a, bin_ids)
+            return carry
+
+        lax.fori_loop(0, zs // chunk, part, 0)
+
+    def image(x, start, length):
         def part(i, carry):
             z = start + i * chunk
-            if step == 0:
-                bin_ids = [bins[x, z + j] for j in range(chunk)]
-                total = [jnp.zeros((chunk, ROWS, LANES), F32)] * n_ang
-            else:
-                total = [acc[a, x, pl.ds(z, chunk)] for a in range(n_ang)]
+            bin_ids = [bins[x, z + j] for j in range(chunk)]
+            total = [jnp.zeros((chunk, ROWS, LANES), F32)] * n_ang
             for h in range(n_off):
                 lag = lags[h]
-                product = (
-                    win[step, 0, x, pl.ds(z, chunk), pl.ds(2 * ROWS - lag, ROWS), :]
-                    * win[step, 1, x, pl.ds(z, chunk), pl.ds(2 * ROWS + lag, ROWS), :]
-                )
+                product = 0.0
+                for step in range(steps):
+                    product = product + (
+                        win[step, 0, x, pl.ds(z, chunk), pl.ds(2 * ROWS - lag, ROWS), :]
+                        * win[step, 1, x, pl.ds(z, chunk), pl.ds(2 * ROWS + lag, ROWS), :]
+                    )
                 for a in range(n_ang):
-                    if step == 0:
-                        row = table[h, a]
-                        weight = jnp.stack([jnp.take_along_axis(row, bin_ids[j], axis=0) for j in range(chunk)])
-                        cache[h, a, x, pl.ds(z, chunk)] = weight
-                    else:
-                        weight = cache[h, a, x, pl.ds(z, chunk)]
+                    weight = cache[h, a, x, pl.ds(z, chunk)] if a < kept else gathered(h, a, bin_ids)
                     total[a] = total[a] + weight * product
             for a in range(n_ang):
-                if step + 1 == steps:
-                    out[a, pl.ds(z, chunk), :, x * LANES : (x + 1) * LANES] = total[a].astype(BF16)
-                else:
-                    acc[a, x, pl.ds(z, chunk)] = total[a]
+                out[a, pl.ds(z, chunk), :, x * LANES : (x + 1) * LANES] = total[a].astype(BF16)
             return carry
 
         lax.fori_loop(0, length // chunk, part, 0)
@@ -373,12 +381,6 @@
     for x in range(halves):
         copies[("bins", x)].wait()
 
-    for x in range(halves):
-        for copy in halo[x]:
-            copy.wait_recv()
-        halo_rows(hw, x, recv0[x, 0].astype(F32), recv0[x, 1].astype(F32))
-        along_y(hw, x, False)
-        finish(0, x, send1)
     def direct(send, recv, send_sems, recv_sems, cells):
         for parity, here in enumerate((jnp.logical_not(odd), odd)):
 
@@ -416,10 +418,17 @@
             for index in range(len(PASSED)):
                 passed(recv, send_sems[3:], recv_sems, cells, index).wait_send()
 
-    everything = (pl.ds(0, halves),)
-    first_sems = [send_sem1.at[i] for i in range(5)], [recv_sem1.at[i] for i in range(4)]
-    direct(send1, recv1, *first_sems, everything)
-
+    first_sems = [
+        ([send_sem1.at[5 * x + i] for i in range(5)], [recv_sem1.at[4 * x + i] for i in range(4)]) for x in range(halves)
+    ]
+
+    for x in range(halves):
+        for copy in halo[x]:
+            copy.wait_recv()
+        halo_rows(hw, x, recv0[x, 0].astype(F32), recv0[x, 1].astype(F32))
+        along_y(hw, x, False)
+        finish(0, x, send1)
+        direct(send1, recv1, *first_sems[x], (x,))
     local_part(1)
     for copy in coefs:
         copy.wait_recv()
@@ -440,16 +449,20 @@
             if x_of == x:
                 direct(send2, recv2, *last_sems[index], cells_of[index])
 
-    collect(0, recv1, *first_sems, everything, range(halves), 0, zs)
-    for x in range(halves):
-        image(0, x, 0, zs)
+    for x in range(halves):
+        keep_weights(x)
+    for x in range(halves):
+        collect(0, recv1, *first_sems[x], (x,), (x,), 0, zs)
     for index, (x, z) in enumerate(pieces):
         collect(1, recv2, *last_sems[index], cells_of[index], (x,), z, length)
-        image(1, x, z, length)
+        if index:
+            image(*pieces[index - 1], length)
+    image(*pieces[-1], length)
 
     for copy in coefs + sum([list(c) for c in halo + partial], []):
         copy.wait_send()
-    sent(send1, recv1, *first_sems, everything)
+    for x in range(halves):
+        sent(send1, recv1, *first_sems[x], (x,))
     for index in range(len(pieces)):
         sent(send2, recv2, *last_sems[index], cells_of[index])
 
@@ -489,7 +502,7 @@
             pltpu.VMEM((receivers // LANES, LANES), jnp.int32),
             pltpu.VMEM((steps, receivers), F32),
             pltpu.VMEM((n_off, n_ang, n_bin, LANES), F32),
-            pltpu.VMEM((n_off, n_ang) + half, F32),
+            pltpu.VMEM((n_off, KEPT) + half, F32),
             pltpu.VMEM((steps, 2, halves, ROWS, LANES), F32),
             pltpu.VMEM((2,) + half, F32),
             pltpu.VMEM((2, halves, zs + 2 * PAD, ROWS, LANES), F32),
@@ -507,7 +520,6 @@
             pltpu.VMEM((4,) + block, BF16),
             pltpu.VMEM((4,) + block, BF16),
             pltpu.VMEM((steps, 2, halves, zs, 5 * ROWS, LANES), F32),
-            pltpu.VMEM((n_ang,) + half, F32),
             dma((8 * halves + 6,)),
             dma((2 * halves,)),
             dma((2 * halves,)),
@@ -515,8 +527,8 @@
             dma((2,)),
             dma((2 * halves,)),
             dma((2 * halves,)),
-            dma((5,)),
-            dma((4,)),
+            dma((5 * halves,)),
+            dma((4 * halves,)),
             dma((5 * halves * PIECES,)),
             dma((4 * halves * PIECES,)),
         ],

time: 37.5 us -> 37.2 us (level)
  Pallas kernels: 36.7 us -> 36.3 us
where the time goes in v5:
time: 37.2 us; the launch traced here: 37.1 us
  Pallas kernels  36.3 us (98%)
  local copies, waits for them, and re-layouts  0.71 us (2%)
    pallas_call x1, Pallas kernels, per_device(): pl.pallas_call(kernel, out_shape=pltpu.VMEM((n_ang, zs, rows, width), BF1...  36.3 us

profile of v5, /device:TPU:513, one launch (start us, length us, event | category | flops | bytes accessed | tf_op | source)
XLA Modules:
  0.0 37.1 jit_solution(480639078742770708)
XLA Ops:
  0.0 36.3 %shard_map.136 = bf16[4,16,8,256]{3,2,1,0:T(8,128)(2,1)S(1)} custom-call(f32[16,8,256]{2,1,0:T(8,128)} %sn_hbm.1, f32[16,8,256]{2,1,0:T(8,128)} %sb_hbm.1, f32[16,8,256]{2,1,0:T(8,128)} %rn_hbm.1, f32[16,8,256]{2,1,0:T(8,128)} %rb_hbm.1, f32[16,8,256]{2,1,0:T(8,128)} %speed_hbm.1, f32[16,8,256]{2,1,0:T(8,128)} %aniso_hbm.1, f32[16,8,256]{2,1,0:T(8,128)} %tilt_hbm.1, ...), custom_call_target="tpu_custom_call" | custom-call | tf_op jit(solution)/shard_map/pallas_call | solution.py:486
  36.4 0.7 %copy.16 = bf16[4,16,8,256]{3,2,1,0:T(8,128)(2,1)} copy(bf16[4,16,8,256]{3,2,1,0:T(8,128)(2,1)S(1)} %shard_map.136) | data formatting | bytes 524288

commit v6 on v5

--- a/solution.py
+++ b/solution.py
@@ -19,6 +19,7 @@
 OFFSETS = (-2, -1, 1, 2)
 DIRECT = ((2, -1, 1), (2, -2, -1))
 PASSED = ((1, 2), (-2, -1))
+GROUP = 8
 KEPT = 4
 PIECES = 2
 
@@ -29,7 +30,7 @@
     out,
     pw, qv, speed, a1, a2, bins, wt, lags, scells, swave, rcells, rtraces, table, cache, inj, base, grad,
     hw, share2, share1, send0, sendc, sendp, send1, send2, recv0, recvc, recvp, recv1, recv2, win,
-    in_sem, send_sem0, recv_sem0, send_semc, recv_semc, send_semp, recv_semp, send_sem1, recv_sem1, send_sem2, recv_sem2,
+    in_sem, beyond, send_sem0, recv_sem0, send_semc, recv_semc, send_semp, recv_semp, send_sem1, recv_sem1, send_sem2, recv_sem2,
 ):
     n = lax.axis_size("gy")
     me = lax.axis_index("gy")
@@ -46,7 +47,7 @@
     inner = pl.ds(PAD, zs)
 
     barrier = pltpu.get_barrier_semaphore()
-    for d in OFFSETS:
+    for d in (1, -1):
         pl.semaphore_signal(barrier, inc=1, device_id={"gy": peer[d]}, device_id_type=MESH)
 
     copies = {}
@@ -155,7 +156,7 @@
             copies[("now", m, x)].wait()
         pack(pw[0, 0, x, inner, own, :], pw[0, 1, x, inner, own, :], send0, x, pl.ds(0, zs))
         if x == 0:
-            pl.semaphore_wait(barrier, len(OFFSETS))
+            pl.semaphore_wait(barrier, 2)
         for copy in halo[x]:
             copy.start()
 
@@ -321,23 +322,31 @@
         def part(i, carry):
             z = start + i * chunk
             bin_ids = [bins[x, z + j] for j in range(chunk)]
-            total = [jnp.zeros((chunk, ROWS, LANES), F32)] * n_ang
-            for h in range(n_off):
-                lag = lags[h]
-                product = 0.0
-                for step in range(steps):
-                    product = product + (
-                        win[step, 0, x, pl.ds(z, chunk), pl.ds(2 * ROWS - lag, ROWS), :]
-                        * win[step, 1, x, pl.ds(z, chunk), pl.ds(2 * ROWS + lag, ROWS), :]
-                    )
-                for a in range(n_ang):
-                    weight = cache[h, a, x, pl.ds(z, chunk)] if a < kept else gathered(h, a, bin_ids)
-                    total[a] = total[a] + weight * product
+            def lag_group(g, total):
+                total = list(total)
+                for j in range(GROUP):
+                    h = g * GROUP + j
+                    lag = lags[h]
+                    product = 0.0
+                    for step in range(steps):
+                        product = product + (
+                            win[step, 0, x, pl.ds(z, chunk), pl.ds(2 * ROWS - lag, ROWS), :]
+                            * win[step, 1, x, pl.ds(z, chunk), pl.ds(2 * ROWS + lag, ROWS), :]
+                        )
+                    for a in range(n_ang):
+                        weight = cache[h, a, x, pl.ds(z, chunk)] if a < kept else gathered(h, a, bin_ids)
+                        total[a] = total[a] + weight * product
+                return tuple(total)
+
+            total = lax.fori_loop(0, n_off // GROUP, lag_group, (jnp.zeros((chunk, ROWS, LANES), F32),) * n_ang)
             for a in range(n_ang):
                 out[a, pl.ds(z, chunk), :, x * LANES : (x + 1) * LANES] = total[a].astype(BF16)
             return carry
 
         lax.fori_loop(0, length // chunk, part, 0)
+
+    for d in (1, -1):
+        pl.semaphore_signal(beyond, inc=1, device_id={"gy": peer[d]}, device_id_type=MESH)
 
     injections()
     for x in range(halves):
@@ -428,6 +437,8 @@
         halo_rows(hw, x, recv0[x, 0].astype(F32), recv0[x, 1].astype(F32))
         along_y(hw, x, False)
         finish(0, x, send1)
+        if x == 0:
+            pl.semaphore_wait(beyond, 2)
         direct(send1, recv1, *first_sems[x], (x,))
     local_part(1)
     for copy in coefs:
@@ -521,6 +532,7 @@
             pltpu.VMEM((4,) + block, BF16),
             pltpu.VMEM((steps, 2, halves, zs, 5 * ROWS, LANES), F32),
             dma((8 * halves + 6,)),
+            pltpu.SemaphoreType.REGULAR,
             dma((2 * halves,)),
             dma((2 * halves,)),
             dma((2,)),

time: 37.2 us -> 37.3 us (level)
  no operation moved by 1% of the time
where the time goes in v6:
time: 37.3 us; the launch traced here: 37.2 us
  Pallas kernels  36.5 us (98%)
  local copies, waits for them, and re-layouts  0.71 us (2%)
    pallas_call x1, Pallas kernels, per_device(): pl.pallas_call(kernel, out_shape=pltpu.VMEM((n_ang, zs, rows, width), BF1...  36.5 us

profile of v6, /device:TPU:513, one launch (start us, length us, event | category | flops | bytes accessed | tf_op | source)
XLA Modules:
  0.0 37.2 jit_solution(13782229454141422279)
XLA Ops:
  0.0 36.5 %shard_map.136 = bf16[4,16,8,256]{3,2,1,0:T(8,128)(2,1)S(1)} custom-call(f32[16,8,256]{2,1,0:T(8,128)} %sn_hbm.1, f32[16,8,256]{2,1,0:T(8,128)} %sb_hbm.1, f32[16,8,256]{2,1,0:T(8,128)} %rn_hbm.1, f32[16,8,256]{2,1,0:T(8,128)} %rb_hbm.1, f32[16,8,256]{2,1,0:T(8,128)} %speed_hbm.1, f32[16,8,256]{2,1,0:T(8,128)} %aniso_hbm.1, f32[16,8,256]{2,1,0:T(8,128)} %tilt_hbm.1, ...), custom_call_target="tpu_custom_call" | custom-call | tf_op jit(solution)/shard_map/pallas_call | solution.py:497
  36.5 0.7 %copy.16 = bf16[4,16,8,256]{3,2,1,0:T(8,128)(2,1)} copy(bf16[4,16,8,256]{3,2,1,0:T(8,128)(2,1)S(1)} %shard_map.136) | data formatting | bytes 524288

commit v7 on v6

--- a/solution.py
+++ b/solution.py
@@ -21,7 +21,7 @@
 PASSED = ((1, 2), (-2, -1))
 GROUP = 8
 KEPT = 4
-PIECES = 2
+PIECES = 1
 
 
 def kernel(
@@ -30,7 +30,7 @@
     out,
     pw, qv, speed, a1, a2, bins, wt, lags, scells, swave, rcells, rtraces, table, cache, inj, base, grad,
     hw, share2, share1, send0, sendc, sendp, send1, send2, recv0, recvc, recvp, recv1, recv2, win,
-    in_sem, beyond, send_sem0, recv_sem0, send_semc, recv_semc, send_semp, recv_semp, send_sem1, recv_sem1, send_sem2, recv_sem2,
+    in_sem, send_sem0, recv_sem0, send_semc, recv_semc, send_semp, recv_semp, recv_sem1, recv_sem2,
 ):
     n = lax.axis_size("gy")
     me = lax.axis_index("gy")
@@ -47,7 +47,7 @@
     inner = pl.ds(PAD, zs)
 
     barrier = pltpu.get_barrier_semaphore()
-    for d in (1, -1):
+    for d in OFFSETS:
         pl.semaphore_signal(barrier, inc=1, device_id={"gy": peer[d]}, device_id_type=MESH)
 
     copies = {}
@@ -156,7 +156,7 @@
             copies[("now", m, x)].wait()
         pack(pw[0, 0, x, inner, own, :], pw[0, 1, x, inner, own, :], send0, x, pl.ds(0, zs))
         if x == 0:
-            pl.semaphore_wait(barrier, 2)
+            pl.semaphore_wait(barrier, len(OFFSETS))
         for copy in halo[x]:
             copy.start()
 
@@ -345,9 +345,6 @@
 
         lax.fori_loop(0, length // chunk, part, 0)
 
-    for d in (1, -1):
-        pl.semaphore_signal(beyond, inc=1, device_id={"gy": peer[d]}, device_id_type=MESH)
-
     injections()
     for x in range(halves):
         copies[("speed", x)].wait()
@@ -428,7 +425,7 @@
                 passed(recv, send_sems[3:], recv_sems, cells, index).wait_send()
 
     first_sems = [
-        ([send_sem1.at[5 * x + i] for i in range(5)], [recv_sem1.at[4 * x + i] for i in range(4)]) for x in range(halves)
+        ([in_sem.at[5 * x + i] for i in range(5)], [recv_sem1.at[4 * x + i] for i in range(4)]) for x in range(halves)
     ]
 
     for x in range(halves):
@@ -437,8 +434,6 @@
         halo_rows(hw, x, recv0[x, 0].astype(F32), recv0[x, 1].astype(F32))
         along_y(hw, x, False)
         finish(0, x, send1)
-        if x == 0:
-            pl.semaphore_wait(beyond, 2)
         direct(send1, recv1, *first_sems[x], (x,))
     local_part(1)
     for copy in coefs:
@@ -447,7 +442,7 @@
     pieces = [(x, p * length) for x in range(halves) for p in range(PIECES)]
     cells_of = [(x, slice(None), pl.ds(z, length)) for x, z in pieces]
     last_sems = [
-        ([send_sem2.at[5 * index + i] for i in range(5)], [recv_sem2.at[4 * index + i] for i in range(4)])
+        ([in_sem.at[5 * (halves + index) + i] for i in range(5)], [recv_sem2.at[4 * index + i] for i in range(4)])
         for index in range(len(pieces))
     ]
     for x in range(halves):
@@ -466,9 +461,7 @@
         collect(0, recv1, *first_sems[x], (x,), (x,), 0, zs)
     for index, (x, z) in enumerate(pieces):
         collect(1, recv2, *last_sems[index], cells_of[index], (x,), z, length)
-        if index:
-            image(*pieces[index - 1], length)
-    image(*pieces[-1], length)
+        image(x, z, length)
 
     for copy in coefs + sum([list(c) for c in halo + partial], []):
         copy.wait_send()
@@ -532,16 +525,13 @@
             pltpu.VMEM((4,) + block, BF16),
             pltpu.VMEM((steps, 2, halves, zs, 5 * ROWS, LANES), F32),
             dma((8 * halves + 6,)),
-            pltpu.SemaphoreType.REGULAR,
             dma((2 * halves,)),
             dma((2 * halves,)),
             dma((2,)),
             dma((2,)),
             dma((2 * halves,)),
             dma((2 * halves,)),
-            dma((5 * halves,)),
             dma((4 * halves,)),
-            dma((5 * halves * PIECES,)),
             dma((4 * halves * PIECES,)),
         ],
         compiler_params=pltpu.CompilerParams(collective_id=0, has_side_effects=True),

time: 37.3 us -> 36.6 us (0.981)
  Pallas kernels: 36.5 us -> 35.7 us
    pallas_call x1, Pallas kernels: 36.5 us -> 35.7 us  [per_device(): pl.pallas_call(kernel, out_shape=pltpu.VMEM((n_ang, zs, rows, width), BF1...]
where the time goes in v7:
time: 36.6 us; the launch traced here: 36.4 us
  Pallas kernels  35.7 us (98%)
  local copies, waits for them, and re-layouts  0.71 us (2%)
    pallas_call x1, Pallas kernels, per_device(): pl.pallas_call(kernel, out_shape=pltpu.VMEM((n_ang, zs, rows, width), BF1...  35.7 us

profile of v7, /device:TPU:513, one launch (start us, length us, event | category | flops | bytes accessed | tf_op | source)
XLA Modules:
  0.0 36.4 jit_solution(5585517226707424525)
XLA Ops:
  0.0 35.7 %shard_map.136 = bf16[4,16,8,256]{3,2,1,0:T(8,128)(2,1)S(1)} custom-call(f32[16,8,256]{2,1,0:T(8,128)} %sn_hbm.1, f32[16,8,256]{2,1,0:T(8,128)} %sb_hbm.1, f32[16,8,256]{2,1,0:T(8,128)} %rn_hbm.1, f32[16,8,256]{2,1,0:T(8,128)} %rb_hbm.1, f32[16,8,256]{2,1,0:T(8,128)} %speed_hbm.1, f32[16,8,256]{2,1,0:T(8,128)} %aniso_hbm.1, f32[16,8,256]{2,1,0:T(8,128)} %tilt_hbm.1, ...), custom_call_target="tpu_custom_call" | custom-call | tf_op jit(solution)/shard_map/pallas_call | solution.py:490
  35.7 0.7 %copy.16 = bf16[4,16,8,256]{3,2,1,0:T(8,128)(2,1)} copy(bf16[4,16,8,256]{3,2,1,0:T(8,128)(2,1)S(1)} %shard_map.136) | data formatting | bytes 524288

commit v8 on v7

--- a/solution.py
+++ b/solution.py
@@ -29,7 +29,7 @@
     lags_hbm, scells_hbm, swave_hbm, rcells_hbm, rtraces_hbm,
     out,
     pw, qv, speed, a1, a2, bins, wt, lags, scells, swave, rcells, rtraces, table, cache, inj, base, grad,
-    hw, share2, share1, send0, sendc, sendp, send1, send2, recv0, recvc, recvp, recv1, recv2, win,
+    hw, share2, share1, send0, sendc, sendp, send1, send2, recv0, recvc, recvp, recv1, recv2, win, acc,
     in_sem, send_sem0, recv_sem0, send_semc, recv_semc, send_semp, recv_semp, recv_sem1, recv_sem2,
 ):
     n = lax.axis_size("gy")
@@ -318,7 +318,7 @@
 
         lax.fori_loop(0, zs // chunk, part, 0)
 
-    def image(x, start, length):
+    def image(step, x, start, length):
         def part(i, carry):
             z = start + i * chunk
             bin_ids = [bins[x, z + j] for j in range(chunk)]
@@ -327,20 +327,24 @@
                 for j in range(GROUP):
                     h = g * GROUP + j
                     lag = lags[h]
-                    product = 0.0
-                    for step in range(steps):
-                        product = product + (
-                            win[step, 0, x, pl.ds(z, chunk), pl.ds(2 * ROWS - lag, ROWS), :]
-                            * win[step, 1, x, pl.ds(z, chunk), pl.ds(2 * ROWS + lag, ROWS), :]
-                        )
+                    product = (
+                        win[step, 0, x, pl.ds(z, chunk), pl.ds(2 * ROWS - lag, ROWS), :]
+                        * win[step, 1, x, pl.ds(z, chunk), pl.ds(2 * ROWS + lag, ROWS), :]
+                    )
                     for a in range(n_ang):
                         weight = cache[h, a, x, pl.ds(z, chunk)] if a < kept else gathered(h, a, bin_ids)
                         total[a] = total[a] + weight * product
                 return tuple(total)
 
-            total = lax.fori_loop(0, n_off // GROUP, lag_group, (jnp.zeros((chunk, ROWS, LANES), F32),) * n_ang)
+            total = tuple(
+                jnp.zeros((chunk, ROWS, LANES), F32) if step == 0 else acc[a, x, pl.ds(z, chunk)] for a in range(n_ang)
+            )
+            total = lax.fori_loop(0, n_off // GROUP, lag_group, total)
             for a in range(n_ang):
-                out[a, pl.ds(z, chunk), :, x * LANES : (x + 1) * LANES] = total[a].astype(BF16)
+                if step + 1 < steps:
+                    acc[a, x, pl.ds(z, chunk)] = total[a]
+                else:
+                    out[a, pl.ds(z, chunk), :, x * LANES : (x + 1) * LANES] = total[a].astype(BF16)
             return carry
 
         lax.fori_loop(0, length // chunk, part, 0)
@@ -459,9 +463,10 @@
         keep_weights(x)
     for x in range(halves):
         collect(0, recv1, *first_sems[x], (x,), (x,), 0, zs)
+        image(0, x, 0, zs)
     for index, (x, z) in enumerate(pieces):
         collect(1, recv2, *last_sems[index], cells_of[index], (x,), z, length)
-        image(x, z, length)
+        image(1, x, z, length)
 
     for copy in coefs + sum([list(c) for c in halo + partial], []):
         copy.wait_send()
@@ -524,6 +529,7 @@
             pltpu.VMEM((4,) + block, BF16),
             pltpu.VMEM((4,) + block, BF16),
             pltpu.VMEM((steps, 2, halves, zs, 5 * ROWS, LANES), F32),
+            pltpu.VMEM((n_ang,) + half, F32),
             dma((8 * halves + 6,)),
             dma((2 * halves,)),
             dma((2 * halves,)),

time: 36.6 us -> 36.5 us (level)
  no operation moved by 1% of the time
where the time goes in v8:
time: 36.5 us; the launch traced here: 36.3 us
  Pallas kernels  35.6 us (98%)
  local copies, waits for them, and re-layouts  0.71 us (2%)
    pallas_call x1, Pallas kernels, per_device(): pl.pallas_call(kernel, out_shape=pltpu.VMEM((n_ang, zs, rows, width), BF1...  35.6 us

profile of v8, /device:TPU:513, one launch (start us, length us, event | category | flops | bytes accessed | tf_op | source)
XLA Modules:
  0.0 36.3 jit_solution(10128497467935678317)
XLA Ops:
  0.0 35.6 %shard_map.136 = bf16[4,16,8,256]{3,2,1,0:T(8,128)(2,1)S(1)} custom-call(f32[16,8,256]{2,1,0:T(8,128)} %sn_hbm.1, f32[16,8,256]{2,1,0:T(8,128)} %sb_hbm.1, f32[16,8,256]{2,1,0:T(8,128)} %rn_hbm.1, f32[16,8,256]{2,1,0:T(8,128)} %rb_hbm.1, f32[16,8,256]{2,1,0:T(8,128)} %speed_hbm.1, f32[16,8,256]{2,1,0:T(8,128)} %aniso_hbm.1, f32[16,8,256]{2,1,0:T(8,128)} %tilt_hbm.1, ...), custom_call_target="tpu_custom_call" | custom-call | tf_op jit(solution)/shard_map/pallas_call | solution.py:495
  35.6 0.7 %copy.16 = bf16[4,16,8,256]{3,2,1,0:T(8,128)(2,1)} copy(bf16[4,16,8,256]{3,2,1,0:T(8,128)(2,1)S(1)} %shard_map.136) | data formatting | bytes 524288

commit v9 on v8

--- a/solution.py
+++ b/solution.py
@@ -379,15 +379,8 @@
         )
         for copy in partial[x]:
             copy.start()
-    for x in range(halves):
-        shares(x)
     copies["wt"].wait()
     copies["lags"].wait()
-    by_bin = [wt[b].astype(F32) for b in range(n_bin)]
-    for a in range(n_ang):
-        rows = jnp.concatenate([v[a : a + 1] for v in by_bin], axis=0)
-        for h in range(n_off):
-            table[h, a] = jnp.broadcast_to(rows[:, h : h + 1], (n_bin, LANES))
     for x in range(halves):
         copies[("bins", x)].wait()
 
@@ -439,6 +432,8 @@
         along_y(hw, x, False)
         finish(0, x, send1)
         direct(send1, recv1, *first_sems[x], (x,))
+    for x in range(halves):
+        shares(x)
     local_part(1)
     for copy in coefs:
         copy.wait_recv()
@@ -459,6 +454,11 @@
             if x_of == x:
                 direct(send2, recv2, *last_sems[index], cells_of[index])
 
+    by_bin = [wt[b].astype(F32) for b in range(n_bin)]
+    for a in range(n_ang):
+        rows = jnp.concatenate([v[a : a + 1] for v in by_bin], axis=0)
+        for h in range(n_off):
+            table[h, a] = jnp.broadcast_to(rows[:, h : h + 1], (n_bin, LANES))
     for x in range(halves):
         keep_weights(x)
     for x in range(halves):

time: 36.5 us -> 36.9 us (1.011)
  Pallas kernels: 35.6 us -> 36.1 us
    pallas_call x1, Pallas kernels: 35.6 us -> 36.1 us  [per_device(): pl.pallas_call(kernel, out_shape=pltpu.VMEM((n_ang, zs, rows, width), BF1...]
where the time goes in v9:
time: 36.9 us; the launch traced here: 36.8 us
  Pallas kernels  36.1 us (98%)
  local copies, waits for them, and re-layouts  0.71 us (2%)
    pallas_call x1, Pallas kernels, per_device(): pl.pallas_call(kernel, out_shape=pltpu.VMEM((n_ang, zs, rows, width), BF1...  36.1 us

profile of v9, /device:TPU:513, one launch (start us, length us, event | category | flops | bytes accessed | tf_op | source)
XLA Modules:
  0.0 36.8 jit_solution(15391503302542074966)
XLA Ops:
  0.0 36.1 %shard_map.136 = bf16[4,16,8,256]{3,2,1,0:T(8,128)(2,1)S(1)} custom-call(f32[16,8,256]{2,1,0:T(8,128)} %sn_hbm.1, f32[16,8,256]{2,1,0:T(8,128)} %sb_hbm.1, f32[16,8,256]{2,1,0:T(8,128)} %rn_hbm.1, f32[16,8,256]{2,1,0:T(8,128)} %rb_hbm.1, f32[16,8,256]{2,1,0:T(8,128)} %speed_hbm.1, f32[16,8,256]{2,1,0:T(8,128)} %aniso_hbm.1, f32[16,8,256]{2,1,0:T(8,128)} %tilt_hbm.1, ...), custom_call_target="tpu_custom_call" | custom-call | tf_op jit(solution)/shard_map/pallas_call | solution.py:495
  36.1 0.7 %copy.16 = bf16[4,16,8,256]{3,2,1,0:T(8,128)(2,1)} copy(bf16[4,16,8,256]{3,2,1,0:T(8,128)(2,1)S(1)} %shard_map.136) | data formatting | bytes 524288
